TPU v7x, 256 devices: a whole 4x4x8 slice. The times are simulated.
256 devices in a mesh: row: 8 (over z), col: 32 (over x, y, core).
Axes of the slice: x: 4, y: 4, z: 8, core: 2. Of those that a mesh axis runs over, the one named last changes fastest.
Arguments:
- tile_values: bfloat16 [8, 32, 128, 128, 128], P('row', 'col'), may hold values from -0.1875 to 0.1875
- tile_rows: int32 [8, 32, 128], P('row', 'col'), may hold values from 0 to 15, as said below
- tile_cols: int32 [8, 32, 128], P('row', 'col'), may hold values from 0 to 15, as said below
- tile_count: int32 [8, 32], P('row', 'col'), may hold values from 42 to 128, as said below
- sinogram: float32 [16384, 128], P('row'), may hold values from -6 to 6
Outputs:
- solution: float32 [65536, 128], P('col')
- residual_estimate: float32 [128], replicated
Inputs may be any that keep to these rules, and one draw needn't show every extreme that they name: On each device the 128 slots name distinct tile positions (tile_rows, tile_cols) of its grid of 16 x 16 tiles. `tile_cols`: see tile_rows. `tile_count`: some device holds 128 tiles in every draw.
All inputs are finite; a program needn't handle non-finite values.
Results may differ from a plain program's by a relative error of at most 0.0019.
Values may be sent and summed in bfloat16 or wider, within the bound.
No kernel may reach another device: no remote copies, remote signals or barrier semaphores. Data moves between devices by JAX's collectives and lax.ppermute only.
A program may use at most 128 MiB of HBM per device.

v0:
```python
import jax
import jax.numpy as jnp
from jax import lax
from jax.sharding import Mesh
from jax.sharding import PartitionSpec as P

TR = 16
TC = 16
ITERS = 3
COL = ("col_0", "col_1", "col_2")
ROW_COL = ("row", "col_0", "col_1", "col_2")


EPSILON = 1e-06


def by_axis(array, axes):
    for axis in axes:
        array = lax.psum(array, axis)
    return array


def in_blocks(array, dim, length):
    before, after = (array.shape[:dim], array.shape[dim + 1 :])
    return jnp.moveaxis(array.reshape(*before, length, -1, *after), dim, 0)


def sum_at_owner(array, axis, dim):
    length = lax.axis_size(axis)
    parts = lax.all_to_all(in_blocks(array, dim, length), axis, 0, 0, tiled=True)
    return jnp.sum(parts, axis=0)


def laid_out(parts, dim):
    shape = list(parts.shape[1:])
    shape[dim] *= parts.shape[0]
    return jnp.moveaxis(parts, 0, dim).reshape(shape)


def copy_for_each(array, axis):
    copies = jnp.broadcast_to(array, (lax.axis_size(axis), *array.shape))
    return lax.all_to_all(copies, axis, split_axis=0, concat_axis=0, tiled=True)


def gathered_copies(array, axis, dim):
    return laid_out(copy_for_each(array, axis), dim)


def column_squares(vec):
    return jnp.sum(vec * vec, axis=0)


def rotation(rho_bar, beta_norm, phi_bar):
    rho_value = jnp.sqrt(rho_bar * rho_bar + beta_norm * beta_norm)
    cosine = rho_bar / rho_value
    sine_value = beta_norm / rho_value
    return (rho_value, cosine, sine_value, cosine * phi_bar, sine_value * phi_bar)


def tile_sweep(
    values, take_index, put_index, live_count, source, out_blocks, transpose, group_bound
):
    tile_size = values.shape[1]
    batch_width = source.shape[1]
    blocks = source.reshape(source.shape[0] // tile_size, tile_size, batch_width)
    targets = jnp.arange(out_blocks, dtype=jnp.int32)
    pattern = "tji,tjz->tiz" if transpose else "tij,tjz->tiz"

    def group_step(group_idx, totals):
        first_slot = group_idx * 16
        chosen_tiles = lax.dynamic_slice_in_dim(values, first_slot, 16, 0)
        take_slots = lax.dynamic_slice_in_dim(take_index, first_slot, 16, 0)
        put_slots = lax.dynamic_slice_in_dim(put_index, first_slot, 16, 0)
        operand = blocks[take_slots]
        products = jnp.einsum(pattern, chosen_tiles, operand, preferred_element_type=jnp.float32)
        live_mask = (first_slot + jnp.arange(16, dtype=jnp.int32) < live_count).astype(jnp.float32)
        onehot = (put_slots[None, :] == targets[:, None]).astype(jnp.float32) * live_mask[None, :]
        return totals + jnp.einsum("rt,tiz->riz", onehot, products, precision=lax.Precision.HIGHEST)

    totals = jnp.zeros((out_blocks, tile_size, batch_width), jnp.float32)
    totals = lax.fori_loop(0, group_bound, group_step, totals)
    return totals.reshape(out_blocks * tile_size, batch_width)


def body(tile_values, tile_rows, tile_cols, tile_count, sinogram):
    values = tile_values[0, 0]
    row_slots = tile_rows[0, 0]
    col_slots = tile_cols[0, 0]
    live_count = tile_count[0, 0]
    group_bound = (live_count + 15) // 16

    def backward(source):
        return tile_sweep(values, row_slots, col_slots, live_count, source, TC, True, group_bound)

    share_rows = sinogram.shape[0] // lax.axis_size(COL)
    ray_share = lax.dynamic_slice_in_dim(sinogram, lax.axis_index(COL) * share_rows, share_rows, 0)

    def grid_total(vec):
        return by_axis(column_squares(vec), ROW_COL)

    def backward_share(full_rays):
        return sum_at_owner(backward(full_rays), "row", 0)

    beta_norm = jnp.sqrt(grid_total(ray_share) + EPSILON)
    ray_vec = ray_share / beta_norm
    voxel_raw = backward_share(sinogram.astype(jnp.bfloat16)) / beta_norm
    alpha_norm = jnp.sqrt(grid_total(voxel_raw) + EPSILON)
    voxel_vec = voxel_raw / alpha_norm
    search_dir = voxel_vec
    solution = jnp.zeros_like(voxel_vec)
    phi_bar = beta_norm
    rho_bar = alpha_norm
    for step_idx in range(ITERS):
        gathered = gathered_copies(voxel_raw.astype(jnp.bfloat16), "row", 0)
        fwd_share = sum_at_owner(
            tile_sweep(values, col_slots, row_slots, live_count, gathered, TR, False, group_bound),
            COL,
            0,
        )
        ray_raw = fwd_share / alpha_norm - alpha_norm * ray_vec
        beta_norm = jnp.sqrt(grid_total(ray_raw) + EPSILON)
        ray_vec = ray_raw / beta_norm
        rho_value, cosine, sine_value, phi_value, phi_bar = rotation(rho_bar, beta_norm, phi_bar)
        solution = solution + phi_value / rho_value * search_dir
        if step_idx + 1 < ITERS:
            gathered_rays = lax.all_gather(ray_raw.astype(jnp.bfloat16), COL, axis=0, tiled=True)
            voxel_raw = backward_share(gathered_rays) / beta_norm - beta_norm * voxel_vec
            alpha_norm = jnp.sqrt(grid_total(voxel_raw) + EPSILON)
            voxel_vec = voxel_raw / alpha_norm
            theta_value = sine_value * alpha_norm
            rho_bar = -cosine * alpha_norm
            search_dir = voxel_vec - theta_value / rho_value * search_dir
    solution = lax.all_gather(solution, "row", axis=0, tiled=True)
    return (solution, phi_bar)


def solution(mesh):
    split = Mesh(
        mesh.devices.reshape(mesh.shape["row"], 4, 4, 2), ("row", "col_0", "col_1", "col_2")
    )
    placed = (
        P("row", COL, None, None, None),
        P("row", COL, None),
        P("row", COL, None),
        P("row", COL),
        P("row", None),
    )
    return jax.shard_map(
        body, mesh=split, in_specs=placed, out_specs=(P(COL, None), P()), check_vma=False
    )
```

profile of v0, /device:TPU:1, one launch (start us, length us, event | category | flops | bytes accessed | tf_op | source)
XLA Modules:
  0.0 753.2 jit_solution(13253027433705133564)
XLA Ops:
  9.2 23.9 %while.66 = (s32[]{:T(128)}, f32[16,128,128]{2,0,1:T(8,128)S(1)}, s32[]{:T(128)}, s32[128]{0:T(128)}, s32[]{:T(128)}, /*index=5*/bf16[128,128,128]{2,1,0:T(8,128...) while((s32[]{:T(128)}, f32[16,128,128]{2,0,1:T(8,128)S(1)}, ...), condition=%wide.region_1.2_spmd.clone, body=%wide.region_0.1_spmd.clone.sunk | while | flops 117704296 | bytes 6296311 | solution.py:81
  34.5 32.5 %all-to-all-start = ((f32[8,256,128]{2,1,0:T(8,128)}), f32[8,256,128]{2,1,0:T(8,128)S(1)}, u32[]{:S(2)}, u32[]{:S(2)}) async-start(f32[8,256,128]{2,1,0:T(8,128)} %bitcast.5), calls=%async_computation | async-start | bytes 2097152 | tf_op jit(solution)/shard_map/all_to_all | solution.py:30
  67.8 32.4 %psum.196 = f32[128]{0:T(128)S(1)} all-reduce(f32[128]{0:T(128)S(1)} %multiply_reduce_fusion.6), channel_id=1, replica_groups=mesh['row'=8,'col_0'=4,'col_1'=4,'col_2'=2] {'row'}, use_global_device_ids=true, to_apply=%region_4.5 | all-reduce | flops 128 | bytes 1024 | tf_op jit(solution)/shard_map/psum | solution.py:19
  100.1 6.3 psum.197
  106.5 8.5 %psum.198 = f32[128]{0:T(128)S(1)} all-reduce(f32[128]{0:T(128)S(1)} %psum.197), channel_id=1, replica_groups=mesh['row'=8,'col_0'=4,'col_1'=4,'col_2'=2] {'col_1'}, use_global_device_ids=true, to_apply=%region_6.7 | all-reduce | flops 128 | bytes 1024 | tf_op jit(solution)/shard_map/psum | solution.py:19
  114.9 9.1 %psum.199 = f32[128]{0:T(128)S(1)} all-reduce(f32[128]{0:T(128)S(1)} %psum.198), channel_id=1, replica_groups=mesh['row'=8,'col_0'=4,'col_1'=4,'col_2'=2] {'col_2'}, use_global_device_ids=true, to_apply=%region_7.8 | all-reduce | flops 128 | bytes 1024 | tf_op jit(solution)/shard_map/psum | solution.py:19
  125.0 5.5 all-to-all-start.1
  130.6 18.0 %all-to-all-done.1 = bf16[8,256,128]{2,1,0:T(8,128)(2,1)S(1)} async-done(((bf16[8,256,128]{2,1,0:T(8,128)(2,1)}), bf16[8,256,128]{2,1,0:T(8,128)(2,1)S(1)}, u32[]{:S(2)}, u32[]{:S(2)}) %all-to-all-start.1) | async-done | bytes 524320 | tf_op jit(solution)/shard_map/all_to_all | solution.py:42
  148.6 18.5 %while.67 = (s32[]{:T(128)}, f32[16,128,128]{2,0,1:T(8,128)S(1)}, s32[]{:T(128)}, s32[128]{0:T(128)S(1)}, s32[]{:T(128)}, /*index=5*/bf16[128,128,128]{2,1,0:T(8...) while((s32[]{:T(128)}, f32[16,128,128]{2,0,1:T(8,128)S(1)}, ...), condition=%wide.region_14.15_spmd.clone, body=%wide.region_13.14_spmd.clone.sunk | while | flops 117704296 | bytes 6296311 | solution.py:81
  168.4 21.6 %all-to-all-start.2 = ((f32[32,64,128]{2,1,0:T(8,128)}), f32[32,64,128]{2,1,0:T(8,128)S(1)}, u32[]{:S(2)}, u32[]{:S(2)}) async-start(f32[32,64,128]{2,1,0:T(8,128)} %bitcast.7), calls=%async_computation.2 | async-start | bytes 2097152 | tf_op jit(solution)/shard_map/all_to_all | solution.py:30
  190.0 11.9 %psum.200 = f32[128]{0:T(128)S(1)} all-reduce(f32[128]{0:T(128)S(1)} %get-tuple-element.522), channel_id=1, replica_groups=mesh['row'=8,'col_0'=4,'col_1'=4,'col_2'=2] {'row'}, use_global_device_ids=true, to_apply=%region_9.10 | all-reduce | flops 128 | bytes 1024 | tf_op jit(solution)/shard_map/psum | solution.py:19
  201.9 8.9 %psum.201 = f32[128]{0:T(128)S(1)} all-reduce(f32[128]{0:T(128)S(1)} %psum.200), channel_id=1, replica_groups=mesh['row'=8,'col_0'=4,'col_1'=4,'col_2'=2] {'col_0'}, use_global_device_ids=true, to_apply=%region_10.11 | all-reduce | flops 128 | bytes 1024 | tf_op jit(solution)/shard_map/psum | solution.py:19
  210.7 8.0 %psum.202 = f32[128]{0:T(128)S(1)} all-reduce(f32[128]{0:T(128)S(1)} %psum.201), channel_id=1, replica_groups=mesh['row'=8,'col_0'=4,'col_1'=4,'col_2'=2] {'col_1'}, use_global_device_ids=true, to_apply=%region_11.12 | all-reduce | flops 128 | bytes 1024 | tf_op jit(solution)/shard_map/psum | solution.py:19
  218.8 8.9 %psum.203 = f32[128]{0:T(128)S(1)} all-reduce(f32[128]{0:T(128)S(1)} %psum.202), channel_id=1, replica_groups=mesh['row'=8,'col_0'=4,'col_1'=4,'col_2'=2] {'col_2'}, use_global_device_ids=true, to_apply=%region_12.13 | all-reduce | flops 128 | bytes 1024 | tf_op jit(solution)/shard_map/psum | solution.py:19
  228.6 22.1 %all_gather.9 = bf16[2048,128]{1,0:T(8,128)(2,1)S(1)} all-gather(bf16[64,128]{1,0:T(8,128)(2,1)S(1)} %convert_element_type.68), channel_id=1, replica_groups=mesh['row'=8,'col_0'=4,'col_1'=4,'col_2'=2] {'col_0','col_1','col_2'}, dimensions={0}, use_global_device_ids=true | all-gather | bytes 540672 | tf_op jit(solution)/shard_map/all_gather | solution.py:126
  250.7 18.9 %while.68 = (s32[]{:T(128)}, f32[16,128,128]{2,0,1:T(8,128)S(1)}, s32[]{:T(128)}, s32[128]{0:T(128)S(1)}, s32[]{:T(128)}, /*index=5*/bf16[128,128,128]{2,1,0:T(8...) while((s32[]{:T(128)}, f32[16,128,128]{2,0,1:T(8,128)S(1)}, ...), condition=%wide.region_22.23_spmd.clone, body=%wide.region_21.22_spmd.clone.sunk | while | flops 117704296 | bytes 6296311 | solution.py:81
  270.9 22.1 %all-to-all-start.3 = ((f32[8,256,128]{2,1,0:T(8,128)}), f32[8,256,128]{2,1,0:T(8,128)S(1)}, u32[]{:S(2)}, u32[]{:S(2)}) async-start(f32[8,256,128]{2,1,0:T(8,128)} %bitcast.9), calls=%async_computation.3 | async-start | bytes 2097152 | tf_op jit(solution)/shard_map/all_to_all | solution.py:30
  293.1 33.2 %psum.204 = f32[128]{0:T(128)S(1)} all-reduce(f32[128]{0:T(128)S(1)} %get-tuple-element.519), channel_id=1, replica_groups=mesh['row'=8,'col_0'=4,'col_1'=4,'col_2'=2] {'row'}, use_global_device_ids=true, to_apply=%region_17.18 | all-reduce | flops 128 | bytes 1024 | tf_op jit(solution)/shard_map/psum | solution.py:19
  326.2 6.7 psum.205
  332.9 8.3 %psum.206 = f32[128]{0:T(128)S(1)} all-reduce(f32[128]{0:T(128)S(1)} %psum.205), channel_id=1, replica_groups=mesh['row'=8,'col_0'=4,'col_1'=4,'col_2'=2] {'col_1'}, use_global_device_ids=true, to_apply=%region_19.20 | all-reduce | flops 128 | bytes 1024 | tf_op jit(solution)/shard_map/psum | solution.py:19
  341.2 9.1 %psum.207 = f32[128]{0:T(128)S(1)} all-reduce(f32[128]{0:T(128)S(1)} %psum.206), channel_id=1, replica_groups=mesh['row'=8,'col_0'=4,'col_1'=4,'col_2'=2] {'col_2'}, use_global_device_ids=true, to_apply=%region_20.21 | all-reduce | flops 128 | bytes 1024 | tf_op jit(solution)/shard_map/psum | solution.py:19
  356.8 18.0 %all-to-all-done.4 = bf16[8,256,128]{2,1,0:T(8,128)(2,1)S(1)} async-done(((bf16[8,256,128]{2,1,0:T(8,128)(2,1)}), bf16[8,256,128]{2,1,0:T(8,128)(2,1)S(1)}, u32[]{:S(2)}, u32[]{:S(2)}) %all-to-all-start.4) | async-done | bytes 524320 | tf_op jit(solution)/shard_map/all_to_all | solution.py:42
  374.8 18.5 %while.69 = (s32[]{:T(128)}, f32[16,128,128]{2,0,1:T(8,128)S(1)}, s32[]{:T(128)}, s32[128]{0:T(128)S(1)}, s32[]{:T(128)}, /*index=5*/bf16[128,128,128]{2,1,0:T(8...) while((s32[]{:T(128)}, f32[16,128,128]{2,0,1:T(8,128)S(1)}, ...), condition=%wide.region_30.31_spmd.clone, body=%wide.region_29.30_spmd.clone.sunk | while | flops 117704296 | bytes 6296311 | solution.py:81
  394.6 21.6 %all-to-all-start.5 = ((f32[32,64,128]{2,1,0:T(8,128)}), f32[32,64,128]{2,1,0:T(8,128)S(1)}, u32[]{:S(2)}, u32[]{:S(2)}) async-start(f32[32,64,128]{2,1,0:T(8,128)} %bitcast.11), calls=%async_computation.5 | async-start | bytes 2097152 | tf_op jit(solution)/shard_map/all_to_all | solution.py:30
  416.2 11.9 %psum.208 = f32[128]{0:T(128)S(1)} all-reduce(f32[128]{0:T(128)S(1)} %get-tuple-element.517), channel_id=1, replica_groups=mesh['row'=8,'col_0'=4,'col_1'=4,'col_2'=2] {'row'}, use_global_device_ids=true, to_apply=%region_25.26 | all-reduce | flops 128 | bytes 1024 | tf_op jit(solution)/shard_map/psum | solution.py:19
  428.1 8.9 %psum.209 = f32[128]{0:T(128)S(1)} all-reduce(f32[128]{0:T(128)S(1)} %psum.208), channel_id=1, replica_groups=mesh['row'=8,'col_0'=4,'col_1'=4,'col_2'=2] {'col_0'}, use_global_device_ids=true, to_apply=%region_26.27 | all-reduce | flops 128 | bytes 1024 | tf_op jit(solution)/shard_map/psum | solution.py:19
  437.0 8.0 %psum.210 = f32[128]{0:T(128)S(1)} all-reduce(f32[128]{0:T(128)S(1)} %psum.209), channel_id=1, replica_groups=mesh['row'=8,'col_0'=4,'col_1'=4,'col_2'=2] {'col_1'}, use_global_device_ids=true, to_apply=%region_27.28 | all-reduce | flops 128 | bytes 1024 | tf_op jit(solution)/shard_map/psum | solution.py:19
  445.0 8.9 %psum.211 = f32[128]{0:T(128)S(1)} all-reduce(f32[128]{0:T(128)S(1)} %psum.210), channel_id=1, replica_groups=mesh['row'=8,'col_0'=4,'col_1'=4,'col_2'=2] {'col_2'}, use_global_device_ids=true, to_apply=%region_28.29 | all-reduce | flops 128 | bytes 1024 | tf_op jit(solution)/shard_map/psum | solution.py:19
  454.0 22.1 %all_gather.10 = bf16[2048,128]{1,0:T(8,128)(2,1)S(1)} all-gather(bf16[64,128]{1,0:T(8,128)(2,1)S(1)} %convert_element_type.70), channel_id=1, replica_groups=mesh['row'=8,'col_0'=4,'col_1'=4,'col_2'=2] {'col_0','col_1','col_2'}, dimensions={0}, use_global_device_ids=true | all-gather | bytes 540672 | tf_op jit(solution)/shard_map/all_gather | solution.py:126
  476.2 18.7 %while.70 = (s32[]{:T(128)}, f32[16,128,128]{2,0,1:T(8,128)S(1)}, s32[]{:T(128)}, s32[128]{0:T(128)S(1)}, s32[]{:T(128)}, /*index=5*/bf16[128,128,128]{2,1,0:T(8...) while((s32[]{:T(128)}, f32[16,128,128]{2,0,1:T(8,128)S(1)}, ...), condition=%wide.region_38.39_spmd.clone, body=%wide.region_37.38_spmd.clone.sunk | while | flops 117704296 | bytes 6296311 | solution.py:81
  496.2 22.1 %all-to-all-start.6 = ((f32[8,256,128]{2,1,0:T(8,128)}), f32[8,256,128]{2,1,0:T(8,128)S(1)}, u32[]{:S(2)}, u32[]{:S(2)}) async-start(f32[8,256,128]{2,1,0:T(8,128)} %bitcast.13), calls=%async_computation.6 | async-start | bytes 2097152 | tf_op jit(solution)/shard_map/all_to_all | solution.py:30
  518.3 33.2 %psum.212 = f32[128]{0:T(128)S(1)} all-reduce(f32[128]{0:T(128)S(1)} %get-tuple-element.515), channel_id=1, replica_groups=mesh['row'=8,'col_0'=4,'col_1'=4,'col_2'=2] {'row'}, use_global_device_ids=true, to_apply=%region_33.34 | all-reduce | flops 128 | bytes 1024 | tf_op jit(solution)/shard_map/psum | solution.py:19
  551.5 6.7 psum.213
  558.2 8.2 %psum.214 = f32[128]{0:T(128)S(1)} all-reduce(f32[128]{0:T(128)S(1)} %psum.213), channel_id=1, replica_groups=mesh['row'=8,'col_0'=4,'col_1'=4,'col_2'=2] {'col_1'}, use_global_device_ids=true, to_apply=%region_35.36 | all-reduce | flops 128 | bytes 1024 | tf_op jit(solution)/shard_map/psum | solution.py:19
  566.4 9.1 %psum.215 = f32[128]{0:T(128)S(1)} all-reduce(f32[128]{0:T(128)S(1)} %psum.214), channel_id=1, replica_groups=mesh['row'=8,'col_0'=4,'col_1'=4,'col_2'=2] {'col_2'}, use_global_device_ids=true, to_apply=%region_36.37 | all-reduce | flops 128 | bytes 1024 | tf_op jit(solution)/shard_map/psum | solution.py:19
  576.4 5.6 all-to-all-start.7
  582.0 18.0 %all-to-all-done.7 = bf16[8,256,128]{2,1,0:T(8,128)(2,1)S(1)} async-done(((bf16[8,256,128]{2,1,0:T(8,128)(2,1)}), bf16[8,256,128]{2,1,0:T(8,128)(2,1)S(1)}, u32[]{:S(2)}, u32[]{:S(2)}) %all-to-all-start.7) | async-done | bytes 524320 | tf_op jit(solution)/shard_map/all_to_all | solution.py:42
  600.0 18.7 %while.71 = (s32[]{:T(128)}, f32[16,128,128]{2,0,1:T(8,128)S(1)}, s32[]{:T(128)}, s32[128]{0:T(128)S(1)}, s32[]{:T(128)}, /*index=5*/bf16[128,128,128]{2,1,0:T(8...) while((s32[]{:T(128)}, f32[16,128,128]{2,0,1:T(8,128)S(1)}, ...), condition=%wide.region_46.47_spmd.clone, body=%wide.region_45.46_spmd.clone.sunk | while | flops 117704296 | bytes 6296311 | solution.py:81
  620.0 21.6 %all-to-all-start.8 = ((f32[32,64,128]{2,1,0:T(8,128)}), f32[32,64,128]{2,1,0:T(8,128)S(1)}, u32[]{:S(2)}, u32[]{:S(2)}) async-start(f32[32,64,128]{2,1,0:T(8,128)} %bitcast.15), calls=%async_computation.8 | async-start | bytes 2097152 | tf_op jit(solution)/shard_map/all_to_all | solution.py:30
  641.7 11.9 %psum.216 = f32[128]{0:T(128)S(1)} all-reduce(f32[128]{0:T(128)S(1)} %multiply_reduce_fusion), channel_id=1, replica_groups=mesh['row'=8,'col_0'=4,'col_1'=4,'col_2'=2] {'row'}, use_global_device_ids=true, to_apply=%region_41.42 | all-reduce | flops 128 | bytes 1024 | tf_op jit(solution)/shard_map/psum | solution.py:19
  653.6 8.9 %psum.217 = f32[128]{0:T(128)S(1)} all-reduce(f32[128]{0:T(128)S(1)} %psum.216), channel_id=1, replica_groups=mesh['row'=8,'col_0'=4,'col_1'=4,'col_2'=2] {'col_0'}, use_global_device_ids=true, to_apply=%region_42.43 | all-reduce | flops 128 | bytes 1024 | tf_op jit(solution)/shard_map/psum | solution.py:19
  662.5 7.9 %psum.218 = f32[128]{0:T(128)S(1)} all-reduce(f32[128]{0:T(128)S(1)} %psum.217), channel_id=1, replica_groups=mesh['row'=8,'col_0'=4,'col_1'=4,'col_2'=2] {'col_1'}, use_global_device_ids=true, to_apply=%region_43.44 | all-reduce | flops 128 | bytes 1024 | tf_op jit(solution)/shard_map/psum | solution.py:19
  670.4 9.0 %psum.219 = f32[128]{0:T(128)S(1)} all-reduce(f32[128]{0:T(128)S(1)} %psum.218), channel_id=1, replica_groups=mesh['row'=8,'col_0'=4,'col_1'=4,'col_2'=2] {'col_2'}, use_global_device_ids=true, to_apply=%region_44.45 | all-reduce | flops 128 | bytes 1024 | tf_op jit(solution)/shard_map/psum | solution.py:19
  679.5 12.5 %psum.220 = f32[128]{0:T(128)S(1)} all-reduce(f32[128]{0:T(128)S(1)} %multiply_reduce_fusion.3), channel_id=1, replica_groups=mesh['row'=8,'col_0'=4,'col_1'=4,'col_2'=2] {'row'}, use_global_device_ids=true, to_apply=%region_49.50 | all-reduce | flops 128 | bytes 1024 | tf_op jit(solution)/shard_map/psum | solution.py:19
  692.0 6.0 psum.221
  698.0 6.0 psum.222
  704.0 9.6 %psum.223 = f32[128]{0:T(128)S(1)} all-reduce(f32[128]{0:T(128)S(1)} %psum.222), channel_id=1, replica_groups=mesh['row'=8,'col_0'=4,'col_1'=4,'col_2'=2] {'col_2'}, use_global_device_ids=true, to_apply=%region_52.53 | all-reduce | flops 128 | bytes 1024 | tf_op jit(solution)/shard_map/psum | solution.py:19
  714.9 29.1 %all-gather.2.cloned.1.call-done = f32[2048,128]{1,0:T(8,128)} async-done(((f32[256,128]{1,0:T(8,128)}), f32[2048,128]{1,0:T(8,128)}) %all-gather.2.cloned.1.call-update) | async-done | bytes 1048592 | tf_op jit(solution)/shard_map/all_gather | solution.py:133
  (224 shorter events, 138.9 us)
Async XLA Ops:
  33.2 115.5 %copy-start = (s32[128]{0:T(128)S(1)}, s32[128]{0:T(128)}, u32[]{:S(2)}) copy-start(s32[128]{0:T(128)} %get-tuple-element.1068) | copy-start | bytes 1540
  33.2 115.5 %copy-start.1 = (s32[128]{0:T(128)S(1)}, s32[128]{0:T(128)}, u32[]{:S(2)}) copy-start(s32[128]{0:T(128)} %get-tuple-element.1073) | copy-start | bytes 1540
  34.5 89.6 %all-to-all-start = ((f32[8,256,128]{2,1,0:T(8,128)}), f32[8,256,128]{2,1,0:T(8,128)S(1)}, u32[]{:S(2)}, u32[]{:S(2)}) async-start(f32[8,256,128]{2,1,0:T(8,128)} %bitcast.5), calls=%async_computation | async-start | bytes 2097152 | tf_op jit(solution)/shard_map/all_to_all | solution.py:30
  125.0 23.5 %all-to-all-start.1 = ((bf16[8,256,128]{2,1,0:T(8,128)(2,1)}), bf16[8,256,128]{2,1,0:T(8,128)(2,1)S(1)}, u32[]{:S(2)}, u32[]{:S(2)}) async-start(bf16[8,256,128]{2,1,0:T(8,128)(2,1)} %broadcast_in_dim.26), calls=%async_computation.1 | async-start | bytes 1048576 | tf_op jit(solution)/shard_map/all_to_all | solution.py:42
  168.4 59.3 %all-to-all-start.2 = ((f32[32,64,128]{2,1,0:T(8,128)}), f32[32,64,128]{2,1,0:T(8,128)S(1)}, u32[]{:S(2)}, u32[]{:S(2)}) async-start(f32[32,64,128]{2,1,0:T(8,128)} %bitcast.7), calls=%async_computation.2 | async-start | bytes 2097152 | tf_op jit(solution)/shard_map/all_to_all | solution.py:30
  270.9 79.4 %all-to-all-start.3 = ((f32[8,256,128]{2,1,0:T(8,128)}), f32[8,256,128]{2,1,0:T(8,128)S(1)}, u32[]{:S(2)}, u32[]{:S(2)}) async-start(f32[8,256,128]{2,1,0:T(8,128)} %bitcast.9), calls=%async_computation.3 | async-start | bytes 2097152 | tf_op jit(solution)/shard_map/all_to_all | solution.py:30
  351.3 23.4 %all-to-all-start.4 = ((bf16[8,256,128]{2,1,0:T(8,128)(2,1)}), bf16[8,256,128]{2,1,0:T(8,128)(2,1)S(1)}, u32[]{:S(2)}, u32[]{:S(2)}) async-start(bf16[8,256,128]{2,1,0:T(8,128)(2,1)} %broadcast_in_dim.27), calls=%async_computation.4 | async-start | bytes 1048576 | tf_op jit(solution)/shard_map/all_to_all | solution.py:42
  394.6 59.3 %all-to-all-start.5 = ((f32[32,64,128]{2,1,0:T(8,128)}), f32[32,64,128]{2,1,0:T(8,128)S(1)}, u32[]{:S(2)}, u32[]{:S(2)}) async-start(f32[32,64,128]{2,1,0:T(8,128)} %bitcast.11), calls=%async_computation.5 | async-start | bytes 2097152 | tf_op jit(solution)/shard_map/all_to_all | solution.py:30
  496.2 79.2 %all-to-all-start.6 = ((f32[8,256,128]{2,1,0:T(8,128)}), f32[8,256,128]{2,1,0:T(8,128)S(1)}, u32[]{:S(2)}, u32[]{:S(2)}) async-start(f32[8,256,128]{2,1,0:T(8,128)} %bitcast.13), calls=%async_computation.6 | async-start | bytes 2097152 | tf_op jit(solution)/shard_map/all_to_all | solution.py:30
  576.4 23.6 %all-to-all-start.7 = ((bf16[8,256,128]{2,1,0:T(8,128)(2,1)}), bf16[8,256,128]{2,1,0:T(8,128)(2,1)S(1)}, u32[]{:S(2)}, u32[]{:S(2)}) async-start(bf16[8,256,128]{2,1,0:T(8,128)(2,1)} %broadcast_in_dim.32), calls=%async_computation.7 | async-start | bytes 1048576 | tf_op jit(solution)/shard_map/all_to_all | solution.py:42
  620.0 59.4 %all-to-all-start.8 = ((f32[32,64,128]{2,1,0:T(8,128)}), f32[32,64,128]{2,1,0:T(8,128)S(1)}, u32[]{:S(2)}, u32[]{:S(2)}) async-start(f32[32,64,128]{2,1,0:T(8,128)} %bitcast.15), calls=%async_computation.8 | async-start | bytes 2097152 | tf_op jit(solution)/shard_map/all_to_all | solution.py:30
  641.6 102.5 %all-gather.2.cloned.1.call-start = ((), (), s32[]{:S(2)}) async-start(), calls=%async_computation.9 | async-start | bytes 1179648 | tf_op jit(solution)/shard_map/all_gather | solution.py:133
Sparse Core Ops, SparseCore 0:
  715.1 28.9 all-gather.1
where the time goes:
time: 762 us; the launch traced here: 753 us
  blocking collectives  362 us (48%)
  starting transfers between devices  158 us (21%)
  waiting for transfers between devices  83.1 us (11%)
  matrix products  75.1 us (10%)
  local copies, waits for them, and re-layouts  33 us (4%)
  other arithmetic  25.2 us (3%)
  between operations  14.9 us (2%)
    psum x28, blocking collectives, by_axis(): array = lax.psum(array, axis)  318 us
    all_to_all x6, starting transfers between devices, sum_at_owner(): lax.all_to_all(in_blocks(array, dim, length), axis, 0, 0, tiled=True)  141 us
    all_to_all x3, waiting for transfers between devices, copy_for_each(): return lax.all_to_all(copies, axis, split_axis=0, concat_axis=0, tiled=True)  53.9 us
    all_gather x2, blocking collectives, body(): lax.all_gather(ray_raw.astype(jnp.bfloat16), COL, axis=0, tiled=True)  44.2 us
    dot_general x24, matrix products, group_step(): jnp.einsum('rt,tiz->riz', onehot, products, precision=lax.Precision.HIGHEST)  42.3 us
    dot_general x24, matrix products, group_step(): jnp.einsum(pattern, chosen_tiles, operand, preferred_element_type=jnp.flo...  32.8 us
    all_gather x1, waiting for transfers between devices, body(): solution = lax.all_gather(solution, 'row', axis=0, tiled=True)  29.1 us
    all_to_all x3, starting transfers between devices, copy_for_each(): return lax.all_to_all(copies, axis, split_axis=0, concat_axis=0, tiled=True)  16.6 us
  transfers between devices with their start and end apart: 10, of which 4 were waited for; matrix products, arithmetic and copies ran while one was open for 0% of the time, Pallas kernels for 0%

commit v1 on v0

v1 whole, which is shorter than its diff:
```python
import jax
import jax.numpy as jnp
from jax import lax
from jax.experimental import pallas as pl
from jax.experimental.pallas import tpu as pltpu
from jax.sharding import Mesh
from jax.sharding import PartitionSpec as P

TILE = 128
ITERS = 3
EPSILON = 1e-06
XY = ("col_0", "col_1")
COL = ("col_0", "col_1", "col_2")
ALL = ("row", "col_0", "col_1", "col_2")
STEPS = 32440.0
META = 8

f32 = jnp.float32
bf16 = jnp.bfloat16
i16 = jnp.int16


def exponent_of(largest):
    return jnp.ceil(jnp.log2(jnp.maximum(largest, 1e-30)))


def coded(array, exponent):
    return jnp.round(array * (jnp.exp2(-exponent) * STEPS)).astype(i16)


def step_of(exponent):
    return jnp.exp2(exponent) * (1.0 / STEPS)


def meta_rows(exponent, squares):
    power = exponent_of(squares)
    scaled = squares * jnp.exp2(-power) * 16384.0
    first = jnp.floor(scaled)
    second = jnp.round((scaled - first) * 16384.0)
    blank = jnp.zeros((META - 4, squares.shape[1]), f32)
    return jnp.concatenate([exponent, power, first, second, blank], axis=0).astype(i16)


def squares_in(meta):
    return jnp.exp2(meta[1:2]) * (meta[2:3] + meta[3:4] * (1.0 / 16384.0)) * (1.0 / 16384.0)


def three_pieces(squares):
    high = squares.astype(bf16)
    rest = squares - high.astype(f32)
    middle = rest.astype(bf16)
    low = (rest - middle.astype(f32)).astype(bf16)
    blank = jnp.zeros((META - 3, squares.shape[1]), f32)
    return jnp.concatenate(
        [high.astype(f32), middle.astype(f32), low.astype(f32), blank], axis=0
    ).astype(bf16)


def column_squares(array):
    return jnp.sum(array * array, axis=0, keepdims=True)


def back_project(matrix_ref, rays, part_ref, out_ref, squares):
    voxels = matrix_ref.shape[1]
    rays_t = rays.astype(f32).T.astype(bf16)
    width = 256
    for first in range(0, voxels, width):
        part = jnp.dot(rays_t, matrix_ref[:, first : first + width], preferred_element_type=f32)
        part_ref[first : first + width, :] = part.T
    part = part_ref[...]
    exponent = exponent_of(jnp.max(jnp.abs(part), axis=0, keepdims=True))
    meta = meta_rows(exponent, squares)
    peers = out_ref.shape[0]
    rows = voxels // peers
    codes = coded(part, exponent)
    for peer in range(peers):
        out_ref[peer, :rows, :] = codes[peer * rows : (peer + 1) * rows]
        out_ref[peer, rows : rows + META, :] = meta


def first_kernel(rows_ref, cols_ref, count_ref, tiles_ref, sinogram_ref, matrix_ref, out_ref, part_ref):
    matrix_ref[...] = jnp.zeros(matrix_ref.shape, bf16)

    def place(slot, carry):
        row = pl.multiple_of(rows_ref[slot] * TILE, TILE)
        col = pl.multiple_of(cols_ref[slot] * TILE, TILE)
        matrix_ref[pl.ds(row, TILE), pl.ds(col, TILE)] = tiles_ref[slot]
        return carry

    lax.fori_loop(0, count_ref[0], place, 0)
    sinogram = sinogram_ref[...]
    back_project(matrix_ref, sinogram.astype(bf16), part_ref, out_ref, column_squares(sinogram))


def backward_kernel(core_ref, matrix_ref, own_ref, other_ref, out_ref, rays_ref, part_ref):
    peers = own_ref.shape[0]
    share = own_ref.shape[1] - META
    core = core_ref[0]
    for source_ref, which in ((own_ref, core), (other_ref, 1 - core)):
        for peer in range(peers):
            start = pl.multiple_of(which * (peers * share) + peer * share, share)
            rays_ref[pl.ds(start, share), :] = source_ref[peer, :share, :]

    def pieces(ref):
        total = jnp.zeros((1, ref.shape[2]), f32)
        for peer in range(peers):
            meta = ref[peer, share : share + META, :].astype(f32)
            total = total + (meta[0:1] + meta[1:2] + meta[2:3])
        return total

    squares = pieces(own_ref) + pieces(other_ref)
    back_project(matrix_ref, rays_ref[...], part_ref, out_ref, squares)


def voxel_kernel(*refs, first):
    if first:
        part_ref, out_ref, raw_ref, beta_ref = refs
    else:
        part_ref, raw_before_ref, alpha_ref, out_ref, raw_ref, beta_ref = refs
    peers = part_ref.shape[0]
    rows = part_ref.shape[1] - META
    total = jnp.zeros((rows, part_ref.shape[2]), f32)
    squares = jnp.zeros((1, part_ref.shape[2]), f32)
    for peer in range(peers):
        meta = part_ref[peer, rows : rows + META, :].astype(f32)
        total = total + part_ref[peer, :rows, :].astype(f32) * step_of(meta[0:1])
        squares = squares + squares_in(meta)
    beta = jnp.sqrt(squares + EPSILON)
    raw = total / beta
    if not first:
        raw = raw - beta * (raw_before_ref[...] / alpha_ref[...])
    exponent = exponent_of(jnp.max(jnp.abs(raw), axis=0, keepdims=True))
    codes = coded(raw, exponent)
    meta = meta_rows(exponent, column_squares(raw))
    for peer in range(peers):
        out_ref[peer, :rows, :] = codes
        out_ref[peer, rows : rows + META, :] = meta
    raw_ref[...] = raw
    beta_ref[...] = beta


def forward_kernel(core_ref, matrix_ref, voxels_ref, own_ref, other_ref, squares_ref, operand_ref, part_ref):
    peers = voxels_ref.shape[0]
    rows = voxels_ref.shape[1] - META
    squares = jnp.zeros((1, voxels_ref.shape[2]), f32)
    for peer in range(peers):
        meta = voxels_ref[peer, rows : rows + META, :].astype(f32)
        voxels = voxels_ref[peer, :rows, :].astype(f32) * step_of(meta[0:1])
        operand_ref[peer * rows : (peer + 1) * rows, :] = voxels.astype(bf16)
        squares = squares + squares_in(meta)
    height = 256
    for first in range(0, matrix_ref.shape[0], height):
        part_ref[first : first + height, :] = jnp.dot(
            matrix_ref[first : first + height, :], operand_ref[...], preferred_element_type=f32
        )
    core = core_ref[0]
    half = own_ref.shape[0]
    own_ref[...] = part_ref[pl.ds(pl.multiple_of(core * half, half), half), :]
    other = part_ref[pl.ds(pl.multiple_of((1 - core) * half, half), half), :]
    exponent = exponent_of(jnp.max(jnp.abs(other), axis=0, keepdims=True))
    meta = meta_rows(exponent, squares)
    other_ref[:half, :] = coded(other, exponent)
    other_ref[half : half + META, :] = meta
    squares_ref[...] = squares_in(meta.astype(f32))


def pair_kernel(own_ref, squares_ref, received_ref, out_ref):
    half = own_ref.shape[0]
    peers = out_ref.shape[0]
    share = half // peers
    meta = received_ref[half : half + META, :].astype(f32)
    part = own_ref[...] + received_ref[:half, :].astype(f32) * step_of(meta[0:1])
    squares = squares_ref[...] + squares_in(meta)
    exponent = exponent_of(jnp.max(jnp.abs(part), axis=0, keepdims=True))
    codes = coded(part, exponent)
    meta = meta_rows(exponent, squares)
    for peer in range(peers):
        out_ref[peer, :share, :] = codes[peer * share : (peer + 1) * share]
        out_ref[peer, share : share + META, :] = meta


def ray_kernel(part_ref, ray_before_ref, beta_ref, *out_refs, last):
    peers = part_ref.shape[0]
    share = part_ref.shape[1] - META
    total = jnp.zeros((share, part_ref.shape[2]), f32)
    squares = jnp.zeros((1, part_ref.shape[2]), f32)
    for peer in range(peers):
        meta = part_ref[peer, share : share + META, :].astype(f32)
        total = total + part_ref[peer, :share, :].astype(f32) * step_of(meta[0:1])
        squares = squares + squares_in(meta)
    alpha = jnp.sqrt(squares + EPSILON)
    raw = total / alpha - alpha * (ray_before_ref[...] / beta_ref[...])
    if last:
        squares_ref, alpha_ref = out_refs
        squares_ref[...] = column_squares(raw)
    else:
        out_ref, raw_ref, alpha_ref = out_refs
        pieces = three_pieces(column_squares(raw))
        rounded = raw.astype(bf16)
        for peer in range(peers):
            out_ref[peer, :share, :] = rounded
            out_ref[peer, share : share + META, :] = pieces
        raw_ref[...] = raw
    alpha_ref[...] = alpha


def rotation(rho_bar, beta_norm, phi_bar):
    rho_value = jnp.sqrt(rho_bar * rho_bar + beta_norm * beta_norm)
    cosine = rho_bar / rho_value
    sine_value = beta_norm / rho_value
    return (rho_value, cosine, sine_value, cosine * phi_bar, sine_value * phi_bar)


def last_kernel(voxels0, voxels1, voxels2, alpha0, alpha1, alpha2, beta0, beta1, beta2, beta3, out_ref, phi_ref):
    voxels = (voxels0, voxels1, voxels2)
    alphas = [ref[...] for ref in (alpha0, alpha1, alpha2)]
    betas = [ref[...] for ref in (beta0, beta1, beta2, beta3)]
    phi_bar = betas[0]
    rho_bar = alphas[0]
    steps, turns = [], []
    for step in range(ITERS):
        rho_value, cosine, sine_value, phi_value, phi_bar = rotation(rho_bar, betas[step + 1], phi_bar)
        steps.append(phi_value / rho_value)
        if step + 1 < ITERS:
            turns.append(sine_value * alphas[step + 1] / rho_value)
            rho_bar = -cosine * alphas[step + 1]
    peers = voxels0.shape[0]
    rows = voxels0.shape[1] - META
    for peer in range(peers):
        solution_rows = search_dir = None
        for step in range(ITERS):
            meta = voxels[step][peer, rows : rows + META, :].astype(f32)
            raw = voxels[step][peer, :rows, :].astype(f32) * step_of(meta[0:1])
            voxel_vec = raw / alphas[step]
            if step == 0:
                search_dir = voxel_vec
                solution_rows = steps[0] * search_dir
            else:
                search_dir = voxel_vec - turns[step - 1] * search_dir
                solution_rows = solution_rows + steps[step] * search_dir
        out_ref[peer * rows : (peer + 1) * rows, :] = solution_rows
    phi_ref[...] = phi_bar


def whole(memory=pltpu.VMEM):
    return pl.BlockSpec(memory_space=memory)


def call(kernel, operands, outs, scratch=(), scalars=0, limit=24):
    shapes = [jax.ShapeDtypeStruct(shape, dtype) for shape, dtype in outs]
    return pl.pallas_call(
        kernel,
        in_specs=[whole(pltpu.SMEM)] * scalars + [whole()] * (len(operands) - scalars),
        out_specs=[whole()] * len(outs),
        out_shape=shapes,
        scratch_shapes=[pltpu.VMEM(shape, dtype) for shape, dtype in scratch],
        compiler_params=pltpu.CompilerParams(vmem_limit_bytes=limit * 1024 * 1024),
    )(*operands)


def exchanged(array, axis):
    return lax.all_to_all(array, axis, 0, 0, tiled=True)


def body(tile_values, tile_rows, tile_cols, tile_count, sinogram):
    rays, depth = sinogram.shape
    peers_row = lax.axis_size("row")
    peers_xy = lax.axis_size(XY)
    voxels = rays
    rows = voxels // peers_row
    half = rays // 2
    share = half // peers_xy
    core = lax.axis_index("col_2")
    core_arg = core.astype(jnp.int32).reshape(1)

    def swapped(array):
        return lax.ppermute(array, "col_2", [(0, 1), (1, 0)])

    row_block = ((peers_row, rows + META, depth), i16)
    norm_row = ((1, depth), f32)
    part = ((rays, depth), f32)

    matrix, sent = call(
        first_kernel,
        (tile_rows[0, 0], tile_cols[0, 0], tile_count[0], tile_values[0, 0], sinogram),
        [((rays, voxels), bf16), row_block],
        [part],
        scalars=3,
        limit=40,
    )
    ray_raw = lax.dynamic_slice_in_dim(sinogram, core * half + lax.axis_index(XY) * share, share, 0)
    voxel_raw = None
    alphas, betas, gathered = [], [], []
    for step in range(ITERS):
        received = exchanged(sent, "row")
        before = () if step == 0 else (voxel_raw, alphas[-1])
        copies, voxel_raw, beta = call(
            lambda *refs, first=step == 0: voxel_kernel(*refs, first=first),
            (received, *before),
            [row_block, ((rows, depth), f32), norm_row],
        )
        betas.append(beta)
        gathered.append(exchanged(copies, "row"))
        own, other, squares = call(
            forward_kernel,
            (core_arg, matrix, gathered[-1]),
            [((half, depth), f32), ((half + META, depth), i16), norm_row],
            [((voxels, depth), bf16), part],
            scalars=1,
        )
        (sent,) = call(
            pair_kernel, (own, squares, swapped(other)), [((peers_xy, share + META, depth), i16)]
        )
        received = exchanged(sent, XY)
        last = step + 1 == ITERS
        outs = [norm_row, norm_row]
        if not last:
            outs = [((peers_xy, share + META, depth), bf16), ((share, depth), f32), norm_row]
        results = call(
            lambda *refs, last=last: ray_kernel(*refs, last=last), (received, ray_raw, beta), outs
        )
        alphas.append(results[-1])
        if not last:
            copies, ray_raw = results[:2]
            own_rays = exchanged(copies, XY)
            (sent,) = call(
                backward_kernel,
                (core_arg, matrix, own_rays, swapped(own_rays)),
                [row_block],
                [((rays, depth), bf16), part],
                scalars=1,
            )
    devices = lax.axis_size(ALL)
    squares = exchanged(jnp.broadcast_to(results[0][None], (devices, 1, depth)), ALL)
    betas.append(jnp.sqrt(jnp.sum(squares, axis=0) + EPSILON))
    answer, phi_bar = call(
        last_kernel, (*gathered, *alphas, *betas), [((voxels, depth), f32), norm_row]
    )
    return answer, phi_bar[0]


def solution(mesh):
    split = Mesh(mesh.devices.reshape(mesh.shape["row"], 4, 4, 2), ("row", *COL))
    placed = (
        P("row", COL, None, None, None),
        P("row", COL, None),
        P("row", COL, None),
        P("row", COL),
        P("row", None),
    )
    return jax.shard_map(
        body, mesh=split, in_specs=placed, out_specs=(P(COL, None), P()), check_vma=False
    )
```

time: 762 us -> 261 us (0.34); the launches traced: 753 us -> 260 us
  blocking collectives: 362 us -> 171 us
  starting transfers between devices: 158 us -> 23.1 us
  matrix products: 75.1 us -> 0 us
  waiting for transfers between devices: 83.1 us -> 28.5 us
  other arithmetic: 25.2 us -> 0.06 us
  Pallas kernels: 0 us -> 20.7 us
  local copies, waits for them, and re-layouts: 33 us -> 15.6 us
  between operations: 14.9 us -> 1.41 us
    psum x28 -> x0, blocking collectives: 318 us -> none  [by_axis(): array = lax.psum(array, axis)]
    all_to_all x0 -> x10, blocking collectives: none -> 171 us  [exchanged(): return lax.all_to_all(array, axis, 0, 0, tiled=True)]
    all_to_all x9 -> x2, starting transfers between devices: 158 us -> 11.6 us  [exchanged(): return lax.all_to_all(array, axis, 0, 0, tiled=True)]
    dot_general x48 -> x0, matrix products: 75.1 us -> none  [the longest x24 42.3 us: group_step(): jnp.einsum('rt,tiz->riz', onehot, products, precision=lax.Precision.HIGHEST)]
    all_gather x2 -> x0, blocking collectives: 44.2 us -> none  [body(): lax.all_gather(ray_raw.astype(jnp.bfloat16), COL, axis=0, tiled=True)]
    all_to_all x9 -> x2, waiting for transfers between devices: 53.9 us -> 22.6 us  [exchanged(): return lax.all_to_all(array, axis, 0, 0, tiled=True)]
    all_gather x1 -> x0, waiting for transfers between devices: 29.1 us -> none  [body(): solution = lax.all_gather(solution, 'row', axis=0, tiled=True)]
    pallas_call x0 -> x16, Pallas kernels: none -> 20.7 us  [call(): pl.pallas_call(kernel, in_specs=[whole(pltpu.SMEM)] * scalars + [whole()]...]
  transfers between devices with their start and end apart: 10 -> 7, of which waited for: 4 -> 7; matrix products, arithmetic and copies ran while one was open for 0% -> 0% of each run, Pallas kernels for 0% -> 0%
where the time goes in v1:
time: 261 us; the launch traced here: 260 us
  blocking collectives  171 us (66%)
  waiting for transfers between devices  28.5 us (11%)
  starting transfers between devices  23.1 us (9%)
  Pallas kernels  20.7 us (8%)
  local copies, waits for them, and re-layouts  15.6 us (6%)
    all_to_all x10, blocking collectives, exchanged(): return lax.all_to_all(array, axis, 0, 0, tiled=True)  171 us
    all_to_all x2, waiting for transfers between devices, exchanged(): return lax.all_to_all(array, axis, 0, 0, tiled=True)  22.6 us
    pallas_call x16, Pallas kernels, call(): pl.pallas_call(kernel, in_specs=[whole(pltpu.SMEM)] * scalars + [whole()]...  20.7 us
    unnamed x16, local copies, waits for them, and re-layouts  14.7 us
    all_to_all x2, starting transfers between devices, exchanged(): return lax.all_to_all(array, axis, 0, 0, tiled=True)  11.6 us
    ppermute x5, starting transfers between devices, swapped(): return lax.ppermute(array, 'col_2', [(0, 1), (1, 0)])  11.5 us
    ppermute x5, waiting for transfers between devices, swapped(): return lax.ppermute(array, 'col_2', [(0, 1), (1, 0)])  5.91 us
  transfers between devices with their start and end apart: 7, of which 7 were waited for; matrix products, arithmetic and copies ran while one was open for 0% of the time, Pallas kernels for 0%

profile of v1, /device:TPU:1, one launch (start us, length us, event | category | flops | bytes accessed | tf_op | source)
XLA Modules:
  0.0 260.2 jit_solution(18376512049514496716)
XLA Ops:
  1.3 2.2 copy-done.4
  3.5 1.2 copy-done.5
  4.7 0.7 copy-done.6
  5.3 0.7 copy-done.7
  6.0 3.6 %shard_map.68 = (bf16[2048,2048]{1,0:T(8,128)(2,1)S(1)}, s16[8,264,128]{2,1,0:T(8,128)(2,1)S(1)}) custom-call(s32[128]{0:T(128)S(1)} %bitcast.12, s32[128]{0:T(128)S(1)} %bitcast.13, s32[1]{0:T(128)} %bitcast.10.count_ref, bf16[128,128,128]{2,1,0:T(8,128)(2,1)S(1)} %bitcast.11, f32[2048,128]{1,0:T(8,128)S(1)} %copy-done.5), custom_call_target="tpu_custom_call" | custom-call | tf_op jit(solution)/shard_map/pallas_call | solution.py:251
  9.6 3.3 %copy-done = bf16[2048,2048]{1,0:T(8,128)(2,1)} copy-done((bf16[2048,2048]{1,0:T(8,128)(2,1)}, bf16[2048,2048]{1,0:T(8,128)(2,1)S(1)}, u32[]{:S(2)}) %copy-start) | copy-done | bytes 8388632
  12.9 25.1 %all_to_all.60.refs_0_ = s16[8,264,128]{2,1,0:T(8,128)(2,1)S(1)} all-to-all(s16[8,264,128]{2,1,0:T(8,128)(2,1)S(1)} %get-tuple-element.31), channel_id=1, replica_groups=mesh['row'=8,'col_0'=4,'col_1'=4,'col_2'=2] {'row'}, dimensions={0} | all-to-all | bytes 1081344 | tf_op jit(solution)/shard_map/all_to_all | solution.py:262
  38.0 1.1 shard_map.69
  39.1 3.5 %all-to-all-start.1 = ((s16[8,264,128]{2,1,0:T(8,128)(2,1)}), s16[8,264,128]{2,1,0:T(8,128)(2,1)S(1)}, u32[]{:S(2)}, u32[]{:S(2)}) async-start(s16[8,264,128]{2,1,0:T(8,128)(2,1)} %get-tuple-element.32), calls=%async_computation.1 | async-start | bytes 1081344 | tf_op jit(solution)/shard_map/all_to_all | solution.py:262
  42.6 15.7 %all-to-all-done.1.voxels_ref.voxels0 = s16[8,264,128]{2,1,0:T(8,128)(2,1)S(1)} async-done(((s16[8,264,128]{2,1,0:T(8,128)(2,1)}), s16[8,264,128]{2,1,0:T(8,128)(2,1)S(1)}, u32[]{:S(2)}, u32[]{:S(2)}) %all-to-all-start.1) | async-done | bytes 540704 | tf_op jit(solution)/shard_map/all_to_all | solution.py:262
  58.3 3.4 %copy-done.1 = bf16[2048,2048]{1,0:T(8,128)(2,1)S(1)} copy-done((bf16[2048,2048]{1,0:T(8,128)(2,1)S(1)}, bf16[2048,2048]{1,0:T(8,128)(2,1)}, u32[]{:S(2)}) %copy-start.1) | copy-done | bytes 8388632
  61.7 2.6 shard_map.70
  64.3 3.1 %collective-permute-start = (s16[1032,128]{1,0:T(8,128)(2,1)S(1)}, s16[1032,128]{1,0:T(8,128)(2,1)S(1)}, u32[]{:S(2)}, u32[]{:S(2)}) collective-permute-start(s16[1032,128]{1,0:T(8,128)(2,1)S(1)} %get-tuple-element.36), channel_id=1, source_target_pairs={{0,1},{1,0},{2,3},{3,2},{4,5},{5,4},{6,7},{7,6},{8,9},{9,8},{10,11... | collective-permute-start | bytes 792584 | tf_op jit(solution)/shard_map/ppermute | solution.py:277
  67.4 1.2 collective-permute-done.received_ref
  68.5 0.9 shard_map.71
  69.5 8.0 %all-to-all-start.2 = ((s16[16,72,128]{2,1,0:T(8,128)(2,1)}), s16[16,72,128]{2,1,0:T(8,128)(2,1)S(1)}, u32[]{:S(2)}, u32[]{:S(2)}) async-start(s16[16,72,128]{2,1,0:T(8,128)(2,1)} %shard_map.71), calls=%async_computation.2 | async-start | bytes 589824 | tf_op jit(solution)/shard_map/all_to_all | solution.py:262
  77.6 0.8 constant_dynamic-slice_fusion.refs_1_
  78.3 7.0 %all-to-all-done.2.refs_0_ = s16[16,72,128]{2,1,0:T(8,128)(2,1)S(1)} async-done(((s16[16,72,128]{2,1,0:T(8,128)(2,1)}), s16[16,72,128]{2,1,0:T(8,128)(2,1)S(1)}, u32[]{:S(2)}, u32[]{:S(2)}) %all-to-all-start.2) | async-done | bytes 294944 | tf_op jit(solution)/shard_map/all_to_all | solution.py:262
  85.3 0.1 shard_map.72
  85.4 11.2 %all_to_all.61.own_ref = bf16[16,72,128]{2,1,0:T(8,128)(2,1)S(1)} all-to-all(bf16[16,72,128]{2,1,0:T(8,128)(2,1)S(1)} %get-tuple-element.38), channel_id=1, replica_groups=mesh['row'=8,'col_0'=4,'col_1'=4,'col_2'=2] {'col_0','col_1'}, dimensions={0} | all-to-all | bytes 589824 | tf_op jit(solution)/shard_map/all_to_all | solution.py:262
  96.6 2.9 %collective-permute-start.1 = (bf16[16,72,128]{2,1,0:T(8,128)(2,1)S(1)}, bf16[16,72,128]{2,1,0:T(8,128)(2,1)S(1)}, u32[]{:S(2)}, u32[]{:S(2)}) collective-permute-start(bf16[16,72,128]{2,1,0:T(8,128)(2,1)S(1)} %all_to_all.61.own_ref), channel_id=1, source_target_pairs={{0,1},{1,0},{2,3},{3,2},{4,5},{5,4},{6,7},{7,6},{8,9},{9,8},{10,11... | collective-permute-start | bytes 884744 | tf_op jit(solution)/shard_map/ppermute | solution.py:277
  99.6 1.2 collective-permute-done.1.other_ref
  100.8 3.4 %copy-done.2 = bf16[2048,2048]{1,0:T(8,128)(2,1)S(1)} copy-done((bf16[2048,2048]{1,0:T(8,128)(2,1)S(1)}, bf16[2048,2048]{1,0:T(8,128)(2,1)}, u32[]{:S(2)}) %copy-start.2) | copy-done | bytes 8388632
  104.2 1.7 shard_map.73
  105.9 20.8 %all_to_all.62.refs_0_ = s16[8,264,128]{2,1,0:T(8,128)(2,1)S(1)} all-to-all(s16[8,264,128]{2,1,0:T(8,128)(2,1)S(1)} %shard_map.73), channel_id=1, replica_groups=mesh['row'=8,'col_0'=4,'col_1'=4,'col_2'=2] {'row'}, dimensions={0} | all-to-all | bytes 1081344 | tf_op jit(solution)/shard_map/all_to_all | solution.py:262
  126.7 0.3 shard_map.74
  127.0 20.1 %all_to_all.63.voxels_ref.voxels1 = s16[8,264,128]{2,1,0:T(8,128)(2,1)S(1)} all-to-all(s16[8,264,128]{2,1,0:T(8,128)(2,1)S(1)} %get-tuple-element.41), channel_id=1, replica_groups=mesh['row'=8,'col_0'=4,'col_1'=4,'col_2'=2] {'row'}, dimensions={0} | all-to-all | bytes 1081344 | tf_op jit(solution)/shard_map/all_to_all | solution.py:262
  147.1 2.6 %shard_map.75 = (f32[1024,128]{1,0:T(8,128)S(1)}, s16[1032,128]{1,0:T(8,128)(2,1)S(1)}, f32[1,128]{1,0:T(1,128)S(1)}) custom-call(s32[1]{0:T(128)} %bitcast.4.core_ref, bf16[2048,2048]{1,0:T(8,128)(2,1)S(1)} %copy-done.3, s16[8,264,128]{2,1,0:T(8,128)(2,1)S(1)} %all_to_all.63.voxels_ref.voxels1), custom_call_target="tpu_custom_call" | custom-call | tf_op jit(solution)/shard_map/pallas_call | solution.py:251
  149.7 1.2 collective-permute-start.2
  150.9 1.2 collective-permute-done.2.received_ref
  152.1 0.2 shard_map.76
  152.3 10.9 %all_to_all.64.refs_0_ = s16[16,72,128]{2,1,0:T(8,128)(2,1)S(1)} all-to-all(s16[16,72,128]{2,1,0:T(8,128)(2,1)S(1)} %shard_map.76), channel_id=1, replica_groups=mesh['row'=8,'col_0'=4,'col_1'=4,'col_2'=2] {'col_0','col_1'}, dimensions={0} | all-to-all | bytes 589824 | tf_op jit(solution)/shard_map/all_to_all | solution.py:262
  163.3 0.1 shard_map.77
  163.4 11.2 %all_to_all.65.own_ref = bf16[16,72,128]{2,1,0:T(8,128)(2,1)S(1)} all-to-all(bf16[16,72,128]{2,1,0:T(8,128)(2,1)S(1)} %get-tuple-element.47), channel_id=1, replica_groups=mesh['row'=8,'col_0'=4,'col_1'=4,'col_2'=2] {'col_0','col_1'}, dimensions={0} | all-to-all | bytes 589824 | tf_op jit(solution)/shard_map/all_to_all | solution.py:262
  174.6 2.9 %collective-permute-start.3 = (bf16[16,72,128]{2,1,0:T(8,128)(2,1)S(1)}, bf16[16,72,128]{2,1,0:T(8,128)(2,1)S(1)}, u32[]{:S(2)}, u32[]{:S(2)}) collective-permute-start(bf16[16,72,128]{2,1,0:T(8,128)(2,1)S(1)} %all_to_all.65.own_ref), channel_id=1, source_target_pairs={{0,1},{1,0},{2,3},{3,2},{4,5},{5,4},{6,7},{7,6},{8,9},{9,8},{10,11... | collective-permute-start | bytes 884744 | tf_op jit(solution)/shard_map/ppermute | solution.py:277
  177.5 1.2 collective-permute-done.3.other_ref
  178.8 1.8 shard_map.78
  180.5 20.7 %all_to_all.66.refs_0_ = s16[8,264,128]{2,1,0:T(8,128)(2,1)S(1)} all-to-all(s16[8,264,128]{2,1,0:T(8,128)(2,1)S(1)} %shard_map.78), channel_id=1, replica_groups=mesh['row'=8,'col_0'=4,'col_1'=4,'col_2'=2] {'row'}, dimensions={0} | all-to-all | bytes 1081344 | tf_op jit(solution)/shard_map/all_to_all | solution.py:262
  201.2 0.8 shard_map.79
  202.0 20.0 %all_to_all.67.voxels_ref.voxels2 = s16[8,264,128]{2,1,0:T(8,128)(2,1)S(1)} all-to-all(s16[8,264,128]{2,1,0:T(8,128)(2,1)S(1)} %get-tuple-element.50), channel_id=1, replica_groups=mesh['row'=8,'col_0'=4,'col_1'=4,'col_2'=2] {'row'}, dimensions={0} | all-to-all | bytes 1081344 | tf_op jit(solution)/shard_map/all_to_all | solution.py:262
  222.1 2.6 %shard_map.80 = (f32[1024,128]{1,0:T(8,128)S(1)}, s16[1032,128]{1,0:T(8,128)(2,1)S(1)}, f32[1,128]{1,0:T(1,128)S(1)}) custom-call(s32[1]{0:T(128)} %bitcast.4.core_ref, bf16[2048,2048]{1,0:T(8,128)(2,1)S(1)} %copy-done.3, s16[8,264,128]{2,1,0:T(8,128)(2,1)S(1)} %all_to_all.67.voxels_ref.voxels2), custom_call_target="tpu_custom_call" | custom-call | tf_op jit(solution)/shard_map/pallas_call | solution.py:251
  224.7 1.3 collective-permute-start.4
  226.0 1.2 collective-permute-done.4.received_ref
  227.1 0.2 shard_map.81
  227.4 10.9 %all_to_all.68.refs_0_ = s16[16,72,128]{2,1,0:T(8,128)(2,1)S(1)} all-to-all(s16[16,72,128]{2,1,0:T(8,128)(2,1)S(1)} %shard_map.81), channel_id=1, replica_groups=mesh['row'=8,'col_0'=4,'col_1'=4,'col_2'=2] {'col_0','col_1'}, dimensions={0} | all-to-all | bytes 589824 | tf_op jit(solution)/shard_map/all_to_all | solution.py:262
  238.3 0.1 shard_map.82
  238.5 19.9 %all_to_all.69 = f32[256,1,128]{2,1,0:T(1,128)S(1)} all-to-all(f32[256,1,128]{2,1,0:T(1,128)S(1)} %broadcast_in_dim.9), channel_id=1, replica_groups=mesh['row'=8,'col_0'=4,'col_1'=4,'col_2'=2] {'row','col_0','col_1','col_2'}, dimensions={0} | all-to-all | bytes 262144 | tf_op jit(solution)/shard_map/all_to_all | solution.py:262
  258.4 1.7 shard_map.83
  (12 shorter events, 0.1 us)
Async XLA Ops:
  1.3 2.2 copy-start.4
  3.5 1.2 copy-start.5
  4.7 0.7 copy-start.6
  5.3 0.7 copy-start.7
  9.6 3.3 %copy-start = (bf16[2048,2048]{1,0:T(8,128)(2,1)}, bf16[2048,2048]{1,0:T(8,128)(2,1)S(1)}, u32[]{:S(2)}) copy-start(bf16[2048,2048]{1,0:T(8,128)(2,1)S(1)} %get-tuple-element.33.matrix_ref) | copy-start | bytes 25165828
  39.1 19.2 %all-to-all-start.1 = ((s16[8,264,128]{2,1,0:T(8,128)(2,1)}), s16[8,264,128]{2,1,0:T(8,128)(2,1)S(1)}, u32[]{:S(2)}, u32[]{:S(2)}) async-start(s16[8,264,128]{2,1,0:T(8,128)(2,1)} %get-tuple-element.32), calls=%async_computation.1 | async-start | bytes 1081344 | tf_op jit(solution)/shard_map/all_to_all | solution.py:262
  58.3 3.4 %copy-start.1 = (bf16[2048,2048]{1,0:T(8,128)(2,1)S(1)}, bf16[2048,2048]{1,0:T(8,128)(2,1)}, u32[]{:S(2)}) copy-start(bf16[2048,2048]{1,0:T(8,128)(2,1)} %copy-done) | copy-start | bytes 25165828
  64.3 4.3 %collective-permute-start = (s16[1032,128]{1,0:T(8,128)(2,1)S(1)}, s16[1032,128]{1,0:T(8,128)(2,1)S(1)}, u32[]{:S(2)}, u32[]{:S(2)}) collective-permute-start(s16[1032,128]{1,0:T(8,128)(2,1)S(1)} %get-tuple-element.36), channel_id=1, source_target_pairs={{0,1},{1,0},{2,3},{3,2},{4,5},{5,4},{6,7},{7,6},{8,9},{9,8},{10,11... | collective-permute-start | bytes 792584 | tf_op jit(solution)/shard_map/ppermute | solution.py:277
  69.5 15.8 %all-to-all-start.2 = ((s16[16,72,128]{2,1,0:T(8,128)(2,1)}), s16[16,72,128]{2,1,0:T(8,128)(2,1)S(1)}, u32[]{:S(2)}, u32[]{:S(2)}) async-start(s16[16,72,128]{2,1,0:T(8,128)(2,1)} %shard_map.71), calls=%async_computation.2 | async-start | bytes 589824 | tf_op jit(solution)/shard_map/all_to_all | solution.py:262
  96.6 4.2 %collective-permute-start.1 = (bf16[16,72,128]{2,1,0:T(8,128)(2,1)S(1)}, bf16[16,72,128]{2,1,0:T(8,128)(2,1)S(1)}, u32[]{:S(2)}, u32[]{:S(2)}) collective-permute-start(bf16[16,72,128]{2,1,0:T(8,128)(2,1)S(1)} %all_to_all.61.own_ref), channel_id=1, source_target_pairs={{0,1},{1,0},{2,3},{3,2},{4,5},{5,4},{6,7},{7,6},{8,9},{9,8},{10,11... | collective-permute-start | bytes 884744 | tf_op jit(solution)/shard_map/ppermute | solution.py:277
  100.8 3.4 %copy-start.2 = (bf16[2048,2048]{1,0:T(8,128)(2,1)S(1)}, bf16[2048,2048]{1,0:T(8,128)(2,1)}, u32[]{:S(2)}) copy-start(bf16[2048,2048]{1,0:T(8,128)(2,1)} %copy-done) | copy-start | bytes 25165828
  104.2 42.9 %copy-start.3 = (bf16[2048,2048]{1,0:T(8,128)(2,1)S(1)}, bf16[2048,2048]{1,0:T(8,128)(2,1)}, u32[]{:S(2)}) copy-start(bf16[2048,2048]{1,0:T(8,128)(2,1)} %copy-done) | copy-start | bytes 25165828
  149.7 2.4 collective-permute-start.2
  174.6 4.2 %collective-permute-start.3 = (bf16[16,72,128]{2,1,0:T(8,128)(2,1)S(1)}, bf16[16,72,128]{2,1,0:T(8,128)(2,1)S(1)}, u32[]{:S(2)}, u32[]{:S(2)}) collective-permute-start(bf16[16,72,128]{2,1,0:T(8,128)(2,1)S(1)} %all_to_all.65.own_ref), channel_id=1, source_target_pairs={{0,1},{1,0},{2,3},{3,2},{4,5},{5,4},{6,7},{7,6},{8,9},{9,8},{10,11... | collective-permute-start | bytes 884744 | tf_op jit(solution)/shard_map/ppermute | solution.py:277
  224.7 2.4 collective-permute-start.4

commit v2 on v1

--- a/solution.py
+++ b/solution.py
@@ -14,6 +14,7 @@
 ALL = ("row", "col_0", "col_1", "col_2")
 STEPS = 32440.0
 META = 8
+STAGGER = 7000
 
 f32 = jnp.float32
 bf16 = jnp.bfloat16
@@ -78,18 +79,49 @@
         out_ref[peer, rows : rows + META, :] = meta
 
 
-def first_kernel(rows_ref, cols_ref, count_ref, tiles_ref, sinogram_ref, matrix_ref, out_ref, part_ref):
+def first_kernel(
+    start_ref, count_ref, rows_ref, cols_ref, tiles_ref, sinogram_ref,
+    matrix_ref, out_ref, share_ref,
+    rows_here, cols_here, sinogram_here, part_ref, small_sems, tile_sems,
+):
+    copies = [
+        pltpu.make_async_copy(rows_ref.at[0, 0], rows_here, small_sems.at[0]),
+        pltpu.make_async_copy(cols_ref.at[0, 0], cols_here, small_sems.at[1]),
+        pltpu.make_async_copy(sinogram_ref, sinogram_here, small_sems.at[2]),
+    ]
+    for copy in copies:
+        copy.start()
     matrix_ref[...] = jnp.zeros(matrix_ref.shape, bf16)
-
-    def place(slot, carry):
-        row = pl.multiple_of(rows_ref[slot] * TILE, TILE)
-        col = pl.multiple_of(cols_ref[slot] * TILE, TILE)
-        matrix_ref[pl.ds(row, TILE), pl.ds(col, TILE)] = tiles_ref[slot]
+    copies[0].wait()
+    copies[1].wait()
+    count = count_ref[0]
+
+    def tile_copy(slot):
+        row = pl.multiple_of(rows_here[slot] * TILE, TILE)
+        col = pl.multiple_of(cols_here[slot] * TILE, TILE)
+        target = matrix_ref.at[pl.ds(row, TILE), pl.ds(col, TILE)]
+        return pltpu.make_async_copy(tiles_ref.at[0, 0, slot], target, tile_sems.at[slot])
+
+    def begin(slot, carry):
+        tile_copy(slot).start()
         return carry
 
-    lax.fori_loop(0, count_ref[0], place, 0)
-    sinogram = sinogram_ref[...]
-    back_project(matrix_ref, sinogram.astype(bf16), part_ref, out_ref, column_squares(sinogram))
+    def finish(slot, carry):
+        tile_copy(slot).wait()
+        return carry
+
+    lax.fori_loop(0, count, begin, 0)
+    copies[2].wait()
+    sinogram = sinogram_here[...]
+    squares = column_squares(sinogram)
+    share = share_ref.shape[0]
+    share_ref[...] = sinogram_here[pl.ds(pl.multiple_of(start_ref[0], share), share), :]
+    lax.fori_loop(0, count, finish, 0)
+    back_project(matrix_ref, sinogram.astype(bf16), part_ref, out_ref, squares)
+
+    @pl.when(start_ref[0] >= sinogram.shape[0] // 2)
+    def _():
+        pl.delay(STAGGER)
 
 
 def backward_kernel(core_ref, matrix_ref, own_ref, other_ref, out_ref, rays_ref, part_ref):
@@ -111,12 +143,16 @@
     squares = pieces(own_ref) + pieces(other_ref)
     back_project(matrix_ref, rays_ref[...], part_ref, out_ref, squares)
 
+    @pl.when(core_ref[0] == 1)
+    def _():
+        pl.delay(STAGGER)
+
 
 def voxel_kernel(*refs, first):
     if first:
-        part_ref, out_ref, raw_ref, beta_ref = refs
+        part_ref, out_ref, beta_ref, *raw_refs = refs
     else:
-        part_ref, raw_before_ref, alpha_ref, out_ref, raw_ref, beta_ref = refs
+        part_ref, raw_before_ref, alpha_ref, out_ref, beta_ref, *raw_refs = refs
     peers = part_ref.shape[0]
     rows = part_ref.shape[1] - META
     total = jnp.zeros((rows, part_ref.shape[2]), f32)
@@ -135,11 +171,19 @@
     for peer in range(peers):
         out_ref[peer, :rows, :] = codes
         out_ref[peer, rows : rows + META, :] = meta
-    raw_ref[...] = raw
+    for raw_ref in raw_refs:
+        raw_ref[...] = raw
     beta_ref[...] = beta
 
 
-def forward_kernel(core_ref, matrix_ref, voxels_ref, own_ref, other_ref, squares_ref, operand_ref, part_ref):
+def dense_rows(matrix_ref, start, operand_ref, put):
+    height = 256
+    for first in range(0, matrix_ref.shape[0] // 2, height):
+        rows = pl.ds(pl.multiple_of(start + first, height), height)
+        put(first, jnp.dot(matrix_ref[rows, :], operand_ref[...], preferred_element_type=f32))
+
+
+def forward_kernel(core_ref, matrix_ref, voxels_ref, operand_ref, other_ref, squares_ref, part_ref):
     peers = voxels_ref.shape[0]
     rows = voxels_ref.shape[1] - META
     squares = jnp.zeros((1, voxels_ref.shape[2]), f32)
@@ -148,20 +192,25 @@
         voxels = voxels_ref[peer, :rows, :].astype(f32) * step_of(meta[0:1])
         operand_ref[peer * rows : (peer + 1) * rows, :] = voxels.astype(bf16)
         squares = squares + squares_in(meta)
-    height = 256
-    for first in range(0, matrix_ref.shape[0], height):
-        part_ref[first : first + height, :] = jnp.dot(
-            matrix_ref[first : first + height, :], operand_ref[...], preferred_element_type=f32
-        )
-    core = core_ref[0]
-    half = own_ref.shape[0]
-    own_ref[...] = part_ref[pl.ds(pl.multiple_of(core * half, half), half), :]
-    other = part_ref[pl.ds(pl.multiple_of((1 - core) * half, half), half), :]
+    half = part_ref.shape[0]
+
+    def put(first, part):
+        part_ref[first : first + part.shape[0], :] = part
+
+    dense_rows(matrix_ref, (1 - core_ref[0]) * half, operand_ref, put)
+    other = part_ref[...]
     exponent = exponent_of(jnp.max(jnp.abs(other), axis=0, keepdims=True))
     meta = meta_rows(exponent, squares)
     other_ref[:half, :] = coded(other, exponent)
     other_ref[half : half + META, :] = meta
     squares_ref[...] = squares_in(meta.astype(f32))
+
+
+def own_kernel(core_ref, matrix_ref, operand_ref, own_ref):
+    def put(first, part):
+        own_ref[first : first + part.shape[0], :] = part
+
+    dense_rows(matrix_ref, core_ref[0] * own_ref.shape[0], operand_ref, put)
 
 
 def pair_kernel(own_ref, squares_ref, received_ref, out_ref):
@@ -246,7 +295,7 @@
     return pl.BlockSpec(memory_space=memory)
 
 
-def call(kernel, operands, outs, scratch=(), scalars=0, limit=24):
+def call(kernel, operands, outs, scratch=(), scalars=0, limit=8):
     shapes = [jax.ShapeDtypeStruct(shape, dtype) for shape, dtype in outs]
     return pl.pallas_call(
         kernel,
@@ -280,39 +329,62 @@
     norm_row = ((1, depth), f32)
     part = ((rays, depth), f32)
 
-    matrix, sent = call(
+    start = (core * half + lax.axis_index(XY) * share).astype(jnp.int32).reshape(1)
+    slots = tile_rows.shape[-1]
+    matrix, sent, ray_raw = pl.pallas_call(
         first_kernel,
-        (tile_rows[0, 0], tile_cols[0, 0], tile_count[0], tile_values[0, 0], sinogram),
-        [((rays, voxels), bf16), row_block],
-        [part],
-        scalars=3,
-        limit=40,
+        in_specs=[whole(pltpu.SMEM)] * 2 + [whole(pltpu.HBM)] * 4,
+        out_specs=[whole()] * 3,
+        out_shape=[
+            jax.ShapeDtypeStruct((rays, voxels), bf16),
+            jax.ShapeDtypeStruct(*row_block),
+            jax.ShapeDtypeStruct((share, depth), f32),
+        ],
+        scratch_shapes=[
+            pltpu.SMEM((slots,), jnp.int32),
+            pltpu.SMEM((slots,), jnp.int32),
+            pltpu.VMEM((rays, depth), f32),
+            pltpu.VMEM((rays, depth), f32),
+            pltpu.SemaphoreType.DMA((3,)),
+            pltpu.SemaphoreType.DMA((slots,)),
+        ],
+        compiler_params=pltpu.CompilerParams(vmem_limit_bytes=16 * 1024 * 1024),
+    )(
+        start,
+        tile_count[0],
+        *(
+            pltpu.with_memory_space_constraint(array, pltpu.HBM)
+            for array in (tile_rows, tile_cols, tile_values, sinogram)
+        ),
     )
-    ray_raw = lax.dynamic_slice_in_dim(sinogram, core * half + lax.axis_index(XY) * share, share, 0)
     voxel_raw = None
     alphas, betas, gathered = [], [], []
     for step in range(ITERS):
         received = exchanged(sent, "row")
         before = () if step == 0 else (voxel_raw, alphas[-1])
-        copies, voxel_raw, beta = call(
+        last = step + 1 == ITERS
+        copies, beta, *raw = call(
             lambda *refs, first=step == 0: voxel_kernel(*refs, first=first),
             (received, *before),
-            [row_block, ((rows, depth), f32), norm_row],
+            [row_block, norm_row] + [((rows, depth), f32)] * (not last),
         )
+        if raw:
+            voxel_raw = raw[0]
         betas.append(beta)
         gathered.append(exchanged(copies, "row"))
-        own, other, squares = call(
+        operand, other, squares = call(
             forward_kernel,
             (core_arg, matrix, gathered[-1]),
-            [((half, depth), f32), ((half + META, depth), i16), norm_row],
-            [((voxels, depth), bf16), part],
+            [((voxels, depth), bf16), ((half + META, depth), i16), norm_row],
+            [((half, depth), f32)],
             scalars=1,
         )
+        others = swapped(other)
+        (own,) = call(own_kernel, (core_arg, matrix, operand), [((half, depth), f32)], scalars=1)
         (sent,) = call(
-            pair_kernel, (own, squares, swapped(other)), [((peers_xy, share + META, depth), i16)]
+            pair_kernel, (own, squares, others), [((peers_xy, share + META, depth), i16)]
         )
         received = exchanged(sent, XY)
-        last = step + 1 == ITERS
         outs = [norm_row, norm_row]
         if not last:
             outs = [((peers_xy, share + META, depth), bf16), ((share, depth), f32), norm_row]

time: 261 us -> 230 us (0.88)
  waiting for transfers between devices: 28.5 us -> 3.25 us
  blocking collectives: 171 us -> 191 us
  starting transfers between devices: 23.1 us -> 6.05 us
  local copies, waits for them, and re-layouts: 15.6 us -> 0.07 us
  Pallas kernels: 20.7 us -> 27.7 us
    all_to_all x2 -> x0, waiting for transfers between devices: 22.6 us -> none  [exchanged(): return lax.all_to_all(array, axis, 0, 0, tiled=True)]
    all_to_all x10 -> x12, blocking collectives: 171 us -> 191 us  [exchanged(): return lax.all_to_all(array, axis, 0, 0, tiled=True)]
    unnamed x16 -> x0, local copies, waits for them, and re-layouts: 14.7 us -> none
    pallas_call x0 -> x1, Pallas kernels: none -> 12.4 us  [body(): pl.pallas_call(first_kernel, in_specs=[whole(pltpu.SMEM)] * 2 + [whole(pl...]
    all_to_all x2 -> x0, starting transfers between devices: 11.6 us -> none  [exchanged(): return lax.all_to_all(array, axis, 0, 0, tiled=True)]
    ppermute x5, starting transfers between devices: 11.5 us -> 6.05 us  [swapped(): return lax.ppermute(array, 'col_2', [(0, 1), (1, 0)])]
    pallas_call x16 -> x18, Pallas kernels: 20.7 us -> 15.3 us  [call(): pl.pallas_call(kernel, in_specs=[whole(pltpu.SMEM)] * scalars + [whole()]...]
    ppermute x5, waiting for transfers between devices: 5.91 us -> 3.25 us  [swapped(): return lax.ppermute(array, 'col_2', [(0, 1), (1, 0)])]
  transfers between devices with their start and end apart: 7 -> 5, of which waited for: 7 -> 5; matrix products, arithmetic and copies ran while one was open for 0% -> 0% of each run, Pallas kernels for 0% -> 2%
where the time goes in v2:
time: 230 us
  blocking collectives  191 us (83%)
  Pallas kernels  27.7 us (12%)
  starting transfers between devices  6.05 us (3%)
  waiting for transfers between devices  3.25 us (1%)
    all_to_all x12, blocking collectives, exchanged(): return lax.all_to_all(array, axis, 0, 0, tiled=True)  191 us
    pallas_call x18, Pallas kernels, call(): pl.pallas_call(kernel, in_specs=[whole(pltpu.SMEM)] * scalars + [whole()]...  15.3 us
    pallas_call x1, Pallas kernels, body(): pl.pallas_call(first_kernel, in_specs=[whole(pltpu.SMEM)] * 2 + [whole(pl...  12.4 us
    ppermute x5, starting transfers between devices, swapped(): return lax.ppermute(array, 'col_2', [(0, 1), (1, 0)])  6.05 us
  transfers between devices with their start and end apart: 5, of which 5 were waited for; matrix products, arithmetic and copies ran while one was open for 0% of the time, Pallas kernels for 2%

profile of v2, /device:TPU:1, one launch (start us, length us, event | category | flops | bytes accessed | tf_op | source)
XLA Modules:
  0.0 229.7 jit_solution(13073688832902079191)
XLA Ops:
  1.3 12.4 %shard_map.68 = (bf16[2048,2048]{1,0:T(8,128)(2,1)S(1)}, s16[8,264,128]{2,1,0:T(8,128)(2,1)S(1)}, f32[64,128]{1,0:T(8,128)S(1)}) custom-call(s32[1]{0:T(128)} %bitcast.start_ref, s32[1]{0:T(128)} %bitcast.8.count_ref, s32[1,1,128]{2,1,0:T(1,128)} %rows_ref.1, s32[1,1,128]{2,1,0:T(1,128)} %cols_ref.1, bf16[1,1,128,128,128]{4,3,2,1,0:T(8,128)(2,1)} %tiles_ref.1, ...), custom_call_target="tpu_custom_call" | custom-call | tf_op jit(solution)/shard_map/pallas_call | solution.py:334
  13.7 20.8 %all_to_all.60.refs_0_ = s16[8,264,128]{2,1,0:T(8,128)(2,1)S(1)} all-to-all(s16[8,264,128]{2,1,0:T(8,128)(2,1)S(1)} %get-tuple-element.32), channel_id=1, replica_groups=mesh['row'=8,'col_0'=4,'col_1'=4,'col_2'=2] {'row'}, dimensions={0} | all-to-all | bytes 1081344 | tf_op jit(solution)/shard_map/all_to_all | solution.py:311
  34.6 0.3 shard_map.69
  34.9 16.3 %all_to_all.61.voxels_ref.voxels0 = s16[8,264,128]{2,1,0:T(8,128)(2,1)S(1)} all-to-all(s16[8,264,128]{2,1,0:T(8,128)(2,1)S(1)} %get-tuple-element.33), channel_id=1, replica_groups=mesh['row'=8,'col_0'=4,'col_1'=4,'col_2'=2] {'row'}, dimensions={0} | all-to-all | bytes 1081344 | tf_op jit(solution)/shard_map/all_to_all | solution.py:311
  51.2 1.4 shard_map.70
  52.6 0.1 collective-permute-start
  52.7 1.2 shard_map.71.own_ref
  54.0 0.3 collective-permute-done.received_ref
  54.3 0.2 shard_map.72
  54.5 15.3 %all_to_all.62.refs_0_ = s16[16,72,128]{2,1,0:T(8,128)(2,1)S(1)} all-to-all(s16[16,72,128]{2,1,0:T(8,128)(2,1)S(1)} %shard_map.72), channel_id=1, replica_groups=mesh['row'=8,'col_0'=4,'col_1'=4,'col_2'=2] {'col_0','col_1'}, dimensions={0} | all-to-all | bytes 589824 | tf_op jit(solution)/shard_map/all_to_all | solution.py:311
  69.8 0.1 shard_map.73
  69.9 11.2 %all_to_all.63.own_ref = bf16[16,72,128]{2,1,0:T(8,128)(2,1)S(1)} all-to-all(bf16[16,72,128]{2,1,0:T(8,128)(2,1)S(1)} %get-tuple-element.40), channel_id=1, replica_groups=mesh['row'=8,'col_0'=4,'col_1'=4,'col_2'=2] {'col_0','col_1'}, dimensions={0} | all-to-all | bytes 589824 | tf_op jit(solution)/shard_map/all_to_all | solution.py:311
  81.1 2.8 %collective-permute-start.1 = (bf16[16,72,128]{2,1,0:T(8,128)(2,1)S(1)}, bf16[16,72,128]{2,1,0:T(8,128)(2,1)S(1)}, u32[]{:S(2)}, u32[]{:S(2)}) collective-permute-start(bf16[16,72,128]{2,1,0:T(8,128)(2,1)S(1)} %all_to_all.63.own_ref), channel_id=1, source_target_pairs={{0,1},{1,0},{2,3},{3,2},{4,5},{5,4},{6,7},{7,6},{8,9},{9,8},{10,11... | collective-permute-start | bytes 884744 | tf_op jit(solution)/shard_map/ppermute | solution.py:326
  83.9 1.2 collective-permute-done.1.other_ref
  85.1 1.8 shard_map.74
  86.9 21.7 %all_to_all.64.refs_0_ = s16[8,264,128]{2,1,0:T(8,128)(2,1)S(1)} all-to-all(s16[8,264,128]{2,1,0:T(8,128)(2,1)S(1)} %shard_map.74), channel_id=1, replica_groups=mesh['row'=8,'col_0'=4,'col_1'=4,'col_2'=2] {'row'}, dimensions={0} | all-to-all | bytes 1081344 | tf_op jit(solution)/shard_map/all_to_all | solution.py:311
  108.6 0.3 shard_map.75
  108.9 15.5 %all_to_all.65.voxels_ref.voxels1 = s16[8,264,128]{2,1,0:T(8,128)(2,1)S(1)} all-to-all(s16[8,264,128]{2,1,0:T(8,128)(2,1)S(1)} %get-tuple-element.43), channel_id=1, replica_groups=mesh['row'=8,'col_0'=4,'col_1'=4,'col_2'=2] {'row'}, dimensions={0} | all-to-all | bytes 1081344 | tf_op jit(solution)/shard_map/all_to_all | solution.py:311
  124.4 1.4 shard_map.76
  125.9 0.3 collective-permute-start.2
  126.2 1.2 shard_map.77.own_ref
  127.4 0.3 collective-permute-done.2.received_ref
  127.7 0.2 shard_map.78
  127.9 11.1 %all_to_all.66.refs_0_ = s16[16,72,128]{2,1,0:T(8,128)(2,1)S(1)} all-to-all(s16[16,72,128]{2,1,0:T(8,128)(2,1)S(1)} %shard_map.78), channel_id=1, replica_groups=mesh['row'=8,'col_0'=4,'col_1'=4,'col_2'=2] {'col_0','col_1'}, dimensions={0} | all-to-all | bytes 589824 | tf_op jit(solution)/shard_map/all_to_all | solution.py:311
  139.0 0.1 shard_map.79
  139.1 11.2 %all_to_all.67.own_ref = bf16[16,72,128]{2,1,0:T(8,128)(2,1)S(1)} all-to-all(bf16[16,72,128]{2,1,0:T(8,128)(2,1)S(1)} %get-tuple-element.49), channel_id=1, replica_groups=mesh['row'=8,'col_0'=4,'col_1'=4,'col_2'=2] {'col_0','col_1'}, dimensions={0} | all-to-all | bytes 589824 | tf_op jit(solution)/shard_map/all_to_all | solution.py:311
  150.3 2.8 %collective-permute-start.3 = (bf16[16,72,128]{2,1,0:T(8,128)(2,1)S(1)}, bf16[16,72,128]{2,1,0:T(8,128)(2,1)S(1)}, u32[]{:S(2)}, u32[]{:S(2)}) collective-permute-start(bf16[16,72,128]{2,1,0:T(8,128)(2,1)S(1)} %all_to_all.67.own_ref), channel_id=1, source_target_pairs={{0,1},{1,0},{2,3},{3,2},{4,5},{5,4},{6,7},{7,6},{8,9},{9,8},{10,11... | collective-permute-start | bytes 884744 | tf_op jit(solution)/shard_map/ppermute | solution.py:326
  153.1 1.2 collective-permute-done.3.other_ref
  154.3 1.8 shard_map.80
  156.1 21.7 %all_to_all.68.refs_0_ = s16[8,264,128]{2,1,0:T(8,128)(2,1)S(1)} all-to-all(s16[8,264,128]{2,1,0:T(8,128)(2,1)S(1)} %shard_map.80), channel_id=1, replica_groups=mesh['row'=8,'col_0'=4,'col_1'=4,'col_2'=2] {'row'}, dimensions={0} | all-to-all | bytes 1081344 | tf_op jit(solution)/shard_map/all_to_all | solution.py:311
  177.8 0.3 shard_map.81
  178.1 15.5 %all_to_all.69.voxels_ref.voxels2 = s16[8,264,128]{2,1,0:T(8,128)(2,1)S(1)} all-to-all(s16[8,264,128]{2,1,0:T(8,128)(2,1)S(1)} %get-tuple-element.52), channel_id=1, replica_groups=mesh['row'=8,'col_0'=4,'col_1'=4,'col_2'=2] {'row'}, dimensions={0} | all-to-all | bytes 1081344 | tf_op jit(solution)/shard_map/all_to_all | solution.py:311
  193.6 1.4 shard_map.82
  195.1 0.1 collective-permute-start.4
  195.2 1.2 shard_map.83.own_ref
  196.4 0.3 collective-permute-done.4.received_ref
  196.7 0.2 shard_map.84
  197.0 11.1 %all_to_all.70.refs_0_ = s16[16,72,128]{2,1,0:T(8,128)(2,1)S(1)} all-to-all(s16[16,72,128]{2,1,0:T(8,128)(2,1)S(1)} %shard_map.84), channel_id=1, replica_groups=mesh['row'=8,'col_0'=4,'col_1'=4,'col_2'=2] {'col_0','col_1'}, dimensions={0} | all-to-all | bytes 589824 | tf_op jit(solution)/shard_map/all_to_all | solution.py:311
  208.0 0.1 shard_map.85
  208.2 0.1 broadcast_in_dim.9
  208.2 19.7 %all_to_all.71 = f32[256,1,128]{2,1,0:T(1,128)S(1)} all-to-all(f32[256,1,128]{2,1,0:T(1,128)S(1)} %broadcast_in_dim.9), channel_id=1, replica_groups=mesh['row'=8,'col_0'=4,'col_1'=4,'col_2'=2] {'row','col_0','col_1','col_2'}, dimensions={0} | all-to-all | bytes 262144 | tf_op jit(solution)/shard_map/all_to_all | solution.py:311
  228.0 1.7 shard_map.86
  (2 shorter events, 0.1 us)
Async XLA Ops:
  52.6 1.6 collective-permute-start
  81.1 4.0 %collective-permute-start.1 = (bf16[16,72,128]{2,1,0:T(8,128)(2,1)S(1)}, bf16[16,72,128]{2,1,0:T(8,128)(2,1)S(1)}, u32[]{:S(2)}, u32[]{:S(2)}) collective-permute-start(bf16[16,72,128]{2,1,0:T(8,128)(2,1)S(1)} %all_to_all.63.own_ref), channel_id=1, source_target_pairs={{0,1},{1,0},{2,3},{3,2},{4,5},{5,4},{6,7},{7,6},{8,9},{9,8},{10,11... | collective-permute-start | bytes 884744 | tf_op jit(solution)/shard_map/ppermute | solution.py:326
  125.9 1.8 collective-permute-start.2
  150.3 4.0 %collective-permute-start.3 = (bf16[16,72,128]{2,1,0:T(8,128)(2,1)S(1)}, bf16[16,72,128]{2,1,0:T(8,128)(2,1)S(1)}, u32[]{:S(2)}, u32[]{:S(2)}) collective-permute-start(bf16[16,72,128]{2,1,0:T(8,128)(2,1)S(1)} %all_to_all.67.own_ref), channel_id=1, source_target_pairs={{0,1},{1,0},{2,3},{3,2},{4,5},{5,4},{6,7},{7,6},{8,9},{9,8},{10,11... | collective-permute-start | bytes 884744 | tf_op jit(solution)/shard_map/ppermute | solution.py:326
  195.1 1.6 collective-permute-start.4

commit v3 on v2

--- a/solution.py
+++ b/solution.py
@@ -7,11 +7,13 @@
 from jax.sharding import PartitionSpec as P
 
 TILE = 128
+WIDTH = 256
+CHUNKS = 4
 ITERS = 3
 EPSILON = 1e-06
 XY = ("col_0", "col_1")
 COL = ("col_0", "col_1", "col_2")
-ALL = ("row", "col_0", "col_1", "col_2")
+ROW_XY = ("row", "col_0", "col_1")
 STEPS = 32440.0
 META = 8
 STAGGER = 7000
@@ -61,87 +63,102 @@
     return jnp.sum(array * array, axis=0, keepdims=True)
 
 
-def back_project(matrix_ref, rays, part_ref, out_ref, squares):
-    voxels = matrix_ref.shape[1]
-    rays_t = rays.astype(f32).T.astype(bf16)
-    width = 256
-    for first in range(0, voxels, width):
-        part = jnp.dot(rays_t, matrix_ref[:, first : first + width], preferred_element_type=f32)
-        part_ref[first : first + width, :] = part.T
+def send_parts(part_ref, out_ref, squares):
     part = part_ref[...]
     exponent = exponent_of(jnp.max(jnp.abs(part), axis=0, keepdims=True))
     meta = meta_rows(exponent, squares)
     peers = out_ref.shape[0]
-    rows = voxels // peers
+    rows = part.shape[0] // peers
     codes = coded(part, exponent)
     for peer in range(peers):
         out_ref[peer, :rows, :] = codes[peer * rows : (peer + 1) * rows]
         out_ref[peer, rows : rows + META, :] = meta
+
+
+def transposed(rays):
+    return rays.astype(f32).T.astype(bf16)
 
 
 def first_kernel(
     start_ref, count_ref, rows_ref, cols_ref, tiles_ref, sinogram_ref,
     matrix_ref, out_ref, share_ref,
-    rows_here, cols_here, sinogram_here, part_ref, small_sems, tile_sems,
+    rows_here, cols_here, sinogram_here, tiles_here, rays_ref, part_ref, sems,
 ):
     copies = [
-        pltpu.make_async_copy(rows_ref.at[0, 0], rows_here, small_sems.at[0]),
-        pltpu.make_async_copy(cols_ref.at[0, 0], cols_here, small_sems.at[1]),
-        pltpu.make_async_copy(sinogram_ref, sinogram_here, small_sems.at[2]),
+        pltpu.make_async_copy(rows_ref.at[0, 0], rows_here, sems.at[0]),
+        pltpu.make_async_copy(cols_ref.at[0, 0], cols_here, sems.at[1]),
+        pltpu.make_async_copy(sinogram_ref, sinogram_here, sems.at[2]),
     ]
+    chunk = tiles_here.shape[0] // CHUNKS
+    for index in range(CHUNKS):
+        slots = pl.ds(index * chunk, chunk)
+        source = tiles_ref.at[0, 0, slots]
+        copies.append(pltpu.make_async_copy(source, tiles_here.at[slots], sems.at[3 + index]))
     for copy in copies:
         copy.start()
     matrix_ref[...] = jnp.zeros(matrix_ref.shape, bf16)
-    copies[0].wait()
-    copies[1].wait()
-    count = count_ref[0]
-
-    def tile_copy(slot):
+    for copy in copies[:3]:
+        copy.wait()
+    sinogram = sinogram_here[...]
+    squares = column_squares(sinogram)
+    rays_ref[...] = transposed(sinogram.astype(bf16))
+    share = share_ref.shape[0]
+    share_ref[...] = sinogram_here[pl.ds(pl.multiple_of(start_ref[0], share), share), :]
+
+    def place(slot, carry):
         row = pl.multiple_of(rows_here[slot] * TILE, TILE)
         col = pl.multiple_of(cols_here[slot] * TILE, TILE)
-        target = matrix_ref.at[pl.ds(row, TILE), pl.ds(col, TILE)]
-        return pltpu.make_async_copy(tiles_ref.at[0, 0, slot], target, tile_sems.at[slot])
-
-    def begin(slot, carry):
-        tile_copy(slot).start()
+        matrix_ref[pl.ds(row, TILE), pl.ds(col, TILE)] = tiles_here[slot]
         return carry
 
-    def finish(slot, carry):
-        tile_copy(slot).wait()
-        return carry
-
-    lax.fori_loop(0, count, begin, 0)
-    copies[2].wait()
-    sinogram = sinogram_here[...]
-    squares = column_squares(sinogram)
-    share = share_ref.shape[0]
-    share_ref[...] = sinogram_here[pl.ds(pl.multiple_of(start_ref[0], share), share), :]
-    lax.fori_loop(0, count, finish, 0)
-    back_project(matrix_ref, sinogram.astype(bf16), part_ref, out_ref, squares)
+    for index in range(CHUNKS):
+        copies[3 + index].wait()
+        end = jnp.minimum(count_ref[0], (index + 1) * chunk)
+        lax.fori_loop(index * chunk, end, place, 0)
+    rays_t = rays_ref[...]
+    for first in range(0, matrix_ref.shape[1], WIDTH):
+        part = jnp.dot(rays_t, matrix_ref[:, first : first + WIDTH], preferred_element_type=f32)
+        part_ref[first : first + WIDTH, :] = part.T
+    send_parts(part_ref, out_ref, squares)
 
     @pl.when(start_ref[0] >= sinogram.shape[0] // 2)
     def _():
         pl.delay(STAGGER)
 
 
-def backward_kernel(core_ref, matrix_ref, own_ref, other_ref, out_ref, rays_ref, part_ref):
-    peers = own_ref.shape[0]
-    share = own_ref.shape[1] - META
-    core = core_ref[0]
-    for source_ref, which in ((own_ref, core), (other_ref, 1 - core)):
-        for peer in range(peers):
-            start = pl.multiple_of(which * (peers * share) + peer * share, share)
-            rays_ref[pl.ds(start, share), :] = source_ref[peer, :share, :]
-
-    def pieces(ref):
-        total = jnp.zeros((1, ref.shape[2]), f32)
-        for peer in range(peers):
-            meta = ref[peer, share : share + META, :].astype(f32)
-            total = total + (meta[0:1] + meta[1:2] + meta[2:3])
-        return total
-
-    squares = pieces(own_ref) + pieces(other_ref)
-    back_project(matrix_ref, rays_ref[...], part_ref, out_ref, squares)
+def half_of_rays(source_ref, rays_ref):
+    peers = source_ref.shape[0]
+    share = source_ref.shape[1] - META
+    squares = jnp.zeros((1, source_ref.shape[2]), f32)
+    for peer in range(peers):
+        rays_ref[peer * share : (peer + 1) * share, :] = source_ref[peer, :share, :]
+        meta = source_ref[peer, share : share + META, :].astype(f32)
+        squares = squares + (meta[0:1] + meta[1:2] + meta[2:3])
+    return transposed(rays_ref[...]), squares
+
+
+def half_of_matrix(matrix_ref, which, first):
+    half = matrix_ref.shape[0] // 2
+    start = pl.multiple_of(which * half, half)
+    return matrix_ref[pl.ds(start, half), first : first + WIDTH]
+
+
+def own_backward_kernel(core_ref, matrix_ref, own_ref, sum_ref, squares_ref, rays_ref):
+    rays_t, squares_ref[...] = half_of_rays(own_ref, rays_ref)
+    for first in range(0, matrix_ref.shape[1], WIDTH):
+        sum_ref[:, first : first + WIDTH] = jnp.dot(
+            rays_t, half_of_matrix(matrix_ref, core_ref[0], first), preferred_element_type=f32
+        )
+
+
+def backward_kernel(core_ref, matrix_ref, sum_ref, squares_ref, other_ref, out_ref, rays_ref, part_ref):
+    rays_t, squares = half_of_rays(other_ref, rays_ref)
+    for first in range(0, matrix_ref.shape[1], WIDTH):
+        part = sum_ref[:, first : first + WIDTH] + jnp.dot(
+            rays_t, half_of_matrix(matrix_ref, 1 - core_ref[0], first), preferred_element_type=f32
+        )
+        part_ref[first : first + WIDTH, :] = part.T
+    send_parts(part_ref, out_ref, squares_ref[...] + squares)
 
     @pl.when(core_ref[0] == 1)
     def _():
@@ -344,9 +361,10 @@
             pltpu.SMEM((slots,), jnp.int32),
             pltpu.SMEM((slots,), jnp.int32),
             pltpu.VMEM((rays, depth), f32),
+            pltpu.VMEM(tile_values.shape[2:], bf16),
+            pltpu.VMEM((depth, rays), bf16),
             pltpu.VMEM((rays, depth), f32),
-            pltpu.SemaphoreType.DMA((3,)),
-            pltpu.SemaphoreType.DMA((slots,)),
+            pltpu.SemaphoreType.DMA((3 + CHUNKS,)),
         ],
         compiler_params=pltpu.CompilerParams(vmem_limit_bytes=16 * 1024 * 1024),
     )(
@@ -395,15 +413,24 @@
         if not last:
             copies, ray_raw = results[:2]
             own_rays = exchanged(copies, XY)
+            other_rays = swapped(own_rays)
+            sums, own_squares = call(
+                own_backward_kernel,
+                (core_arg, matrix, own_rays),
+                [((depth, voxels), f32), norm_row],
+                [((half, depth), bf16)],
+                scalars=1,
+            )
             (sent,) = call(
                 backward_kernel,
-                (core_arg, matrix, own_rays, swapped(own_rays)),
+                (core_arg, matrix, sums, own_squares, other_rays),
                 [row_block],
-                [((rays, depth), bf16), part],
+                [((half, depth), bf16), part],
                 scalars=1,
             )
-    devices = lax.axis_size(ALL)
-    squares = exchanged(jnp.broadcast_to(results[0][None], (devices, 1, depth)), ALL)
+    holders = lax.axis_size(ROW_XY)
+    squares = results[0] + swapped(results[0])
+    squares = exchanged(jnp.broadcast_to(squares[None], (holders, 1, depth)), ROW_XY)
     betas.append(jnp.sqrt(jnp.sum(squares, axis=0) + EPSILON))
     answer, phi_bar = call(
         last_kernel, (*gathered, *alphas, *betas), [((voxels, depth), f32), norm_row]

time: 230 us -> 227 us (0.987)
  blocking collectives: 191 us -> 187 us
    all_to_all x12, blocking collectives: 191 us -> 187 us  [exchanged(): return lax.all_to_all(array, axis, 0, 0, tiled=True)]
    ppermute x5 -> x6, starting transfers between devices: 6.05 us -> 8 us  [swapped(): return lax.ppermute(array, 'col_2', [(0, 1), (1, 0)])]
    pallas_call x18 -> x20, Pallas kernels: 15.3 us -> 15.7 us  [call(): pl.pallas_call(kernel, in_specs=[whole(pltpu.SMEM)] * scalars + [whole()]...]
  transfers between devices with their start and end apart: 5 -> 6, of which waited for: 5 -> 6; matrix products, arithmetic and copies ran while one was open for 0% -> 0% of each run, Pallas kernels for 2% -> 2%
where the time goes in v3:
time: 227 us; the launch traced here: 226 us
  blocking collectives  187 us (82%)
  Pallas kernels  27.2 us (12%)
  starting transfers between devices  8 us (4%)
  waiting for transfers between devices  2.47 us (1%)
    all_to_all x12, blocking collectives, exchanged(): return lax.all_to_all(array, axis, 0, 0, tiled=True)  187 us
    pallas_call x20, Pallas kernels, call(): pl.pallas_call(kernel, in_specs=[whole(pltpu.SMEM)] * scalars + [whole()]...  15.7 us
    pallas_call x1, Pallas kernels, body(): pl.pallas_call(first_kernel, in_specs=[whole(pltpu.SMEM)] * 2 + [whole(pl...  11.5 us
    ppermute x6, starting transfers between devices, swapped(): return lax.ppermute(array, 'col_2', [(0, 1), (1, 0)])  8 us
  transfers between devices with their start and end apart: 6, of which 6 were waited for; matrix products, arithmetic and copies ran while one was open for 0% of the time, Pallas kernels for 2%

profile of v3, /device:TPU:1, one launch (start us, length us, event | category | flops | bytes accessed | tf_op | source)
XLA Modules:
  0.0 226.0 jit_solution(15399433952089079844)
XLA Ops:
  1.3 11.5 %shard_map.68 = (bf16[2048,2048]{1,0:T(8,128)(2,1)S(1)}, s16[8,264,128]{2,1,0:T(8,128)(2,1)S(1)}, f32[64,128]{1,0:T(8,128)S(1)}) custom-call(s32[1]{0:T(128)} %bitcast.start_ref, s32[1]{0:T(128)} %bitcast.9.count_ref, s32[1,1,128]{2,1,0:T(1,128)} %rows_ref.1, s32[1,1,128]{2,1,0:T(1,128)} %cols_ref.1, bf16[1,1,128,128,128]{4,3,2,1,0:T(8,128)(2,1)} %tiles_ref.1, ...), custom_call_target="tpu_custom_call" | custom-call | tf_op jit(solution)/shard_map/pallas_call | solution.py:351
  12.8 21.1 %all_to_all.60.refs_0_ = s16[8,264,128]{2,1,0:T(8,128)(2,1)S(1)} all-to-all(s16[8,264,128]{2,1,0:T(8,128)(2,1)S(1)} %get-tuple-element.36), channel_id=1, replica_groups=mesh['row'=8,'col_0'=4,'col_1'=4,'col_2'=2] {'row'}, dimensions={0} | all-to-all | bytes 1081344 | tf_op jit(solution)/shard_map/all_to_all | solution.py:328
  34.0 0.3 shard_map.69
  34.3 15.9 %all_to_all.61.voxels_ref.voxels0 = s16[8,264,128]{2,1,0:T(8,128)(2,1)S(1)} all-to-all(s16[8,264,128]{2,1,0:T(8,128)(2,1)S(1)} %get-tuple-element.37), channel_id=1, replica_groups=mesh['row'=8,'col_0'=4,'col_1'=4,'col_2'=2] {'row'}, dimensions={0} | all-to-all | bytes 1081344 | tf_op jit(solution)/shard_map/all_to_all | solution.py:328
  50.1 1.4 shard_map.70
  51.6 0.1 collective-permute-start
  51.7 1.2 shard_map.71.own_ref
  52.9 0.3 collective-permute-done.received_ref
  53.2 0.2 shard_map.72
  53.5 14.5 %all_to_all.62.refs_0_ = s16[16,72,128]{2,1,0:T(8,128)(2,1)S(1)} all-to-all(s16[16,72,128]{2,1,0:T(8,128)(2,1)S(1)} %shard_map.72), channel_id=1, replica_groups=mesh['row'=8,'col_0'=4,'col_1'=4,'col_2'=2] {'col_0','col_1'}, dimensions={0} | all-to-all | bytes 589824 | tf_op jit(solution)/shard_map/all_to_all | solution.py:328
  68.0 0.1 shard_map.73
  68.1 11.2 %all_to_all.63.own_ref = bf16[16,72,128]{2,1,0:T(8,128)(2,1)S(1)} all-to-all(bf16[16,72,128]{2,1,0:T(8,128)(2,1)S(1)} %get-tuple-element.44), channel_id=1, replica_groups=mesh['row'=8,'col_0'=4,'col_1'=4,'col_2'=2] {'col_0','col_1'}, dimensions={0} | all-to-all | bytes 589824 | tf_op jit(solution)/shard_map/all_to_all | solution.py:328
  79.3 2.8 %collective-permute-start.1 = (bf16[16,72,128]{2,1,0:T(8,128)(2,1)S(1)}, bf16[16,72,128]{2,1,0:T(8,128)(2,1)S(1)}, u32[]{:S(2)}, u32[]{:S(2)}) collective-permute-start(bf16[16,72,128]{2,1,0:T(8,128)(2,1)S(1)} %all_to_all.63.own_ref), channel_id=1, source_target_pairs={{0,1},{1,0},{2,3},{3,2},{4,5},{5,4},{6,7},{7,6},{8,9},{9,8},{10,11... | collective-permute-start | bytes 884744 | tf_op jit(solution)/shard_map/ppermute | solution.py:343
  82.1 0.8 shard_map.74
  82.9 0.4 collective-permute-done.1.other_ref
  83.3 1.2 shard_map.75
  84.5 21.7 %all_to_all.64.refs_0_ = s16[8,264,128]{2,1,0:T(8,128)(2,1)S(1)} all-to-all(s16[8,264,128]{2,1,0:T(8,128)(2,1)S(1)} %shard_map.75), channel_id=1, replica_groups=mesh['row'=8,'col_0'=4,'col_1'=4,'col_2'=2] {'row'}, dimensions={0} | all-to-all | bytes 1081344 | tf_op jit(solution)/shard_map/all_to_all | solution.py:328
  106.2 0.3 shard_map.76
  106.5 15.5 %all_to_all.65.voxels_ref.voxels1 = s16[8,264,128]{2,1,0:T(8,128)(2,1)S(1)} all-to-all(s16[8,264,128]{2,1,0:T(8,128)(2,1)S(1)} %get-tuple-element.49), channel_id=1, replica_groups=mesh['row'=8,'col_0'=4,'col_1'=4,'col_2'=2] {'row'}, dimensions={0} | all-to-all | bytes 1081344 | tf_op jit(solution)/shard_map/all_to_all | solution.py:328
  122.0 1.4 shard_map.77
  123.5 0.3 collective-permute-start.2
  123.8 1.2 shard_map.78.own_ref
  125.0 0.3 collective-permute-done.2.received_ref
  125.3 0.2 shard_map.79
  125.5 11.1 %all_to_all.66.refs_0_ = s16[16,72,128]{2,1,0:T(8,128)(2,1)S(1)} all-to-all(s16[16,72,128]{2,1,0:T(8,128)(2,1)S(1)} %shard_map.79), channel_id=1, replica_groups=mesh['row'=8,'col_0'=4,'col_1'=4,'col_2'=2] {'col_0','col_1'}, dimensions={0} | all-to-all | bytes 589824 | tf_op jit(solution)/shard_map/all_to_all | solution.py:328
  136.6 0.1 shard_map.80
  136.7 11.2 %all_to_all.67.own_ref = bf16[16,72,128]{2,1,0:T(8,128)(2,1)S(1)} all-to-all(bf16[16,72,128]{2,1,0:T(8,128)(2,1)S(1)} %get-tuple-element.55), channel_id=1, replica_groups=mesh['row'=8,'col_0'=4,'col_1'=4,'col_2'=2] {'col_0','col_1'}, dimensions={0} | all-to-all | bytes 589824 | tf_op jit(solution)/shard_map/all_to_all | solution.py:328
  147.9 2.8 %collective-permute-start.3 = (bf16[16,72,128]{2,1,0:T(8,128)(2,1)S(1)}, bf16[16,72,128]{2,1,0:T(8,128)(2,1)S(1)}, u32[]{:S(2)}, u32[]{:S(2)}) collective-permute-start(bf16[16,72,128]{2,1,0:T(8,128)(2,1)S(1)} %all_to_all.67.own_ref), channel_id=1, source_target_pairs={{0,1},{1,0},{2,3},{3,2},{4,5},{5,4},{6,7},{7,6},{8,9},{9,8},{10,11... | collective-permute-start | bytes 884744 | tf_op jit(solution)/shard_map/ppermute | solution.py:343
  150.7 0.8 shard_map.81
  151.5 0.4 collective-permute-done.3.other_ref
  151.9 1.2 shard_map.82
  153.1 21.7 %all_to_all.68.refs_0_ = s16[8,264,128]{2,1,0:T(8,128)(2,1)S(1)} all-to-all(s16[8,264,128]{2,1,0:T(8,128)(2,1)S(1)} %shard_map.82), channel_id=1, replica_groups=mesh['row'=8,'col_0'=4,'col_1'=4,'col_2'=2] {'row'}, dimensions={0} | all-to-all | bytes 1081344 | tf_op jit(solution)/shard_map/all_to_all | solution.py:328
  174.8 0.3 shard_map.83
  175.1 15.5 %all_to_all.69.voxels_ref.voxels2 = s16[8,264,128]{2,1,0:T(8,128)(2,1)S(1)} all-to-all(s16[8,264,128]{2,1,0:T(8,128)(2,1)S(1)} %get-tuple-element.60), channel_id=1, replica_groups=mesh['row'=8,'col_0'=4,'col_1'=4,'col_2'=2] {'row'}, dimensions={0} | all-to-all | bytes 1081344 | tf_op jit(solution)/shard_map/all_to_all | solution.py:328
  190.7 1.4 shard_map.84
  192.1 0.1 collective-permute-start.4
  192.2 1.2 shard_map.85.own_ref
  193.5 0.3 collective-permute-done.4.received_ref
  193.7 0.2 shard_map.86
  194.0 11.1 %all_to_all.70.refs_0_ = s16[16,72,128]{2,1,0:T(8,128)(2,1)S(1)} all-to-all(s16[16,72,128]{2,1,0:T(8,128)(2,1)S(1)} %shard_map.86), channel_id=1, replica_groups=mesh['row'=8,'col_0'=4,'col_1'=4,'col_2'=2] {'col_0','col_1'}, dimensions={0} | all-to-all | bytes 589824 | tf_op jit(solution)/shard_map/all_to_all | solution.py:328
  205.1 0.1 shard_map.87
  205.2 2.0 collective-permute-start.5
  207.1 0.8 collective-permute-done.5
  208.0 16.3 %all_to_all.71 = f32[128,1,128]{2,1,0:T(1,128)S(1)} all-to-all(f32[128,1,128]{2,1,0:T(1,128)S(1)} %broadcast_in_dim.9), channel_id=1, replica_groups=mesh['row'=8,'col_0'=4,'col_1'=4,'col_2'=2] {'row','col_0','col_1'}, dimensions={0} | all-to-all | bytes 131072 | tf_op jit(solution)/shard_map/all_to_all | solution.py:328
  224.3 1.7 shard_map.88
  (4 shorter events, 0.1 us)
Async XLA Ops:
  51.6 1.6 collective-permute-start
  79.3 4.0 %collective-permute-start.1 = (bf16[16,72,128]{2,1,0:T(8,128)(2,1)S(1)}, bf16[16,72,128]{2,1,0:T(8,128)(2,1)S(1)}, u32[]{:S(2)}, u32[]{:S(2)}) collective-permute-start(bf16[16,72,128]{2,1,0:T(8,128)(2,1)S(1)} %all_to_all.63.own_ref), channel_id=1, source_target_pairs={{0,1},{1,0},{2,3},{3,2},{4,5},{5,4},{6,7},{7,6},{8,9},{9,8},{10,11... | collective-permute-start | bytes 884744 | tf_op jit(solution)/shard_map/ppermute | solution.py:343
  123.5 1.8 collective-permute-start.2
  147.9 4.0 %collective-permute-start.3 = (bf16[16,72,128]{2,1,0:T(8,128)(2,1)S(1)}, bf16[16,72,128]{2,1,0:T(8,128)(2,1)S(1)}, u32[]{:S(2)}, u32[]{:S(2)}) collective-permute-start(bf16[16,72,128]{2,1,0:T(8,128)(2,1)S(1)} %all_to_all.67.own_ref), channel_id=1, source_target_pairs={{0,1},{1,0},{2,3},{3,2},{4,5},{5,4},{6,7},{7,6},{8,9},{9,8},{10,11... | collective-permute-start | bytes 884744 | tf_op jit(solution)/shard_map/ppermute | solution.py:343
  192.1 1.6 collective-permute-start.4
  205.2 2.8 %collective-permute-start.5 = (f32[1,128]{1,0:T(1,128)S(1)}, f32[1,128]{1,0:T(1,128)S(1)}, u32[]{:S(2)}, u32[]{:S(2)}) collective-permute-start(f32[1,128]{1,0:T(1,128)S(1)} %get-tuple-element.67), channel_id=1, source_target_pairs={{0,1},{1,0},{2,3},{3,2},{4,5},{5,4},{6,7},{7,6},{8,9},{9,8},{10,11... | collective-permute-start | bytes 1544 | tf_op jit(solution)/shard_map/ppermute | solution.py:343

commit v4 on v3

--- a/solution.py
+++ b/solution.py
@@ -16,7 +16,7 @@
 ROW_XY = ("row", "col_0", "col_1")
 STEPS = 32440.0
 META = 8
-STAGGER = 7000
+STAGGER = 4500
 
 f32 = jnp.float32
 bf16 = jnp.bfloat16
@@ -121,7 +121,7 @@
         part_ref[first : first + WIDTH, :] = part.T
     send_parts(part_ref, out_ref, squares)
 
-    @pl.when(start_ref[0] >= sinogram.shape[0] // 2)
+    @pl.when(start_ref[0] < sinogram.shape[0] // 2)
     def _():
         pl.delay(STAGGER)
 
@@ -160,7 +160,7 @@
         part_ref[first : first + WIDTH, :] = part.T
     send_parts(part_ref, out_ref, squares_ref[...] + squares)
 
-    @pl.when(core_ref[0] == 1)
+    @pl.when(core_ref[0] == 0)
     def _():
         pl.delay(STAGGER)
 

time: 227 us -> 225 us (level)
  starting transfers between devices: 8 us -> 29.1 us
  blocking collectives: 187 us -> 172 us
  Pallas kernels: 27.2 us -> 20.1 us
    ppermute x6, starting transfers between devices: 8 us -> 29.1 us  [swapped(): return lax.ppermute(array, 'col_2', [(0, 1), (1, 0)])]
    all_to_all x12, blocking collectives: 187 us -> 172 us  [exchanged(): return lax.all_to_all(array, axis, 0, 0, tiled=True)]
    pallas_call x1, Pallas kernels: 11.5 us -> 4.42 us  [body(): pl.pallas_call(first_kernel, in_specs=[whole(pltpu.SMEM)] * 2 + [whole(pl...]
  transfers between devices with their start and end apart: 6 -> 6, of which waited for: 6 -> 3; matrix products, arithmetic and copies ran while one was open for 0% -> 0% of each run, Pallas kernels for 2% -> 2%
where the time goes in v4:
time: 225 us
  blocking collectives  172 us (76%)
  starting transfers between devices  29.1 us (13%)
  Pallas kernels  20.1 us (9%)
    all_to_all x12, blocking collectives, exchanged(): return lax.all_to_all(array, axis, 0, 0, tiled=True)  172 us
    ppermute x6, starting transfers between devices, swapped(): return lax.ppermute(array, 'col_2', [(0, 1), (1, 0)])  29.1 us
    pallas_call x20, Pallas kernels, call(): pl.pallas_call(kernel, in_specs=[whole(pltpu.SMEM)] * scalars + [whole()]...  15.7 us
  transfers between devices with their start and end apart: 6, of which 3 were waited for; matrix products, arithmetic and copies ran while one was open for 0% of the time, Pallas kernels for 2%

profile of v4, /device:TPU:1, one launch (start us, length us, event | category | flops | bytes accessed | tf_op | source)
XLA Modules:
  0.0 224.7 jit_solution(17162977042395916967)
XLA Ops:
  1.3 4.4 %shard_map.68 = (bf16[2048,2048]{1,0:T(8,128)(2,1)S(1)}, s16[8,264,128]{2,1,0:T(8,128)(2,1)S(1)}, f32[64,128]{1,0:T(8,128)S(1)}) custom-call(s32[1]{0:T(128)} %bitcast.start_ref, s32[1]{0:T(128)} %bitcast.9.count_ref, s32[1,1,128]{2,1,0:T(1,128)} %rows_ref.1, s32[1,1,128]{2,1,0:T(1,128)} %cols_ref.1, bf16[1,1,128,128,128]{4,3,2,1,0:T(8,128)(2,1)} %tiles_ref.1, ...), custom_call_target="tpu_custom_call" | custom-call | tf_op jit(solution)/shard_map/pallas_call | solution.py:351
  5.7 21.0 %all_to_all.60.refs_0_ = s16[8,264,128]{2,1,0:T(8,128)(2,1)S(1)} all-to-all(s16[8,264,128]{2,1,0:T(8,128)(2,1)S(1)} %get-tuple-element.36), channel_id=1, replica_groups=mesh['row'=8,'col_0'=4,'col_1'=4,'col_2'=2] {'row'}, dimensions={0} | all-to-all | bytes 1081344 | tf_op jit(solution)/shard_map/all_to_all | solution.py:328
  26.7 0.3 shard_map.69
  27.0 14.7 %all_to_all.61.voxels_ref.voxels0 = s16[8,264,128]{2,1,0:T(8,128)(2,1)S(1)} all-to-all(s16[8,264,128]{2,1,0:T(8,128)(2,1)S(1)} %get-tuple-element.37), channel_id=1, replica_groups=mesh['row'=8,'col_0'=4,'col_1'=4,'col_2'=2] {'row'}, dimensions={0} | all-to-all | bytes 1081344 | tf_op jit(solution)/shard_map/all_to_all | solution.py:328
  41.7 1.4 shard_map.70
  43.2 7.8 %collective-permute-start = (s16[1032,128]{1,0:T(8,128)(2,1)S(1)}, s16[1032,128]{1,0:T(8,128)(2,1)S(1)}, u32[]{:S(2)}, u32[]{:S(2)}) collective-permute-start(s16[1032,128]{1,0:T(8,128)(2,1)S(1)} %get-tuple-element.41), channel_id=1, source_target_pairs={{0,1},{1,0},{2,3},{3,2},{4,5},{5,4},{6,7},{7,6},{8,9},{9,8},{10,11... | collective-permute-start | bytes 792584 | tf_op jit(solution)/shard_map/ppermute | solution.py:343
  51.0 1.2 shard_map.71.own_ref
  52.2 0.0 collective-permute-done.received_ref
  52.2 0.2 shard_map.72
  52.5 14.6 %all_to_all.62.refs_0_ = s16[16,72,128]{2,1,0:T(8,128)(2,1)S(1)} all-to-all(s16[16,72,128]{2,1,0:T(8,128)(2,1)S(1)} %shard_map.72), channel_id=1, replica_groups=mesh['row'=8,'col_0'=4,'col_1'=4,'col_2'=2] {'col_0','col_1'}, dimensions={0} | all-to-all | bytes 589824 | tf_op jit(solution)/shard_map/all_to_all | solution.py:328
  67.1 0.1 shard_map.73
  67.2 11.1 %all_to_all.63.own_ref = bf16[16,72,128]{2,1,0:T(8,128)(2,1)S(1)} all-to-all(bf16[16,72,128]{2,1,0:T(8,128)(2,1)S(1)} %get-tuple-element.44), channel_id=1, replica_groups=mesh['row'=8,'col_0'=4,'col_1'=4,'col_2'=2] {'col_0','col_1'}, dimensions={0} | all-to-all | bytes 589824 | tf_op jit(solution)/shard_map/all_to_all | solution.py:328
  78.4 2.9 %collective-permute-start.1 = (bf16[16,72,128]{2,1,0:T(8,128)(2,1)S(1)}, bf16[16,72,128]{2,1,0:T(8,128)(2,1)S(1)}, u32[]{:S(2)}, u32[]{:S(2)}) collective-permute-start(bf16[16,72,128]{2,1,0:T(8,128)(2,1)S(1)} %all_to_all.63.own_ref), channel_id=1, source_target_pairs={{0,1},{1,0},{2,3},{3,2},{4,5},{5,4},{6,7},{7,6},{8,9},{9,8},{10,11... | collective-permute-start | bytes 884744 | tf_op jit(solution)/shard_map/ppermute | solution.py:343
  81.2 0.8 shard_map.74
  82.0 0.4 collective-permute-done.1.other_ref
  82.4 1.2 shard_map.75
  83.6 14.7 %all_to_all.64.refs_0_ = s16[8,264,128]{2,1,0:T(8,128)(2,1)S(1)} all-to-all(s16[8,264,128]{2,1,0:T(8,128)(2,1)S(1)} %shard_map.75), channel_id=1, replica_groups=mesh['row'=8,'col_0'=4,'col_1'=4,'col_2'=2] {'row'}, dimensions={0} | all-to-all | bytes 1081344 | tf_op jit(solution)/shard_map/all_to_all | solution.py:328
  98.3 0.3 shard_map.76
  98.6 15.8 %all_to_all.65.voxels_ref.voxels1 = s16[8,264,128]{2,1,0:T(8,128)(2,1)S(1)} all-to-all(s16[8,264,128]{2,1,0:T(8,128)(2,1)S(1)} %get-tuple-element.49), channel_id=1, replica_groups=mesh['row'=8,'col_0'=4,'col_1'=4,'col_2'=2] {'row'}, dimensions={0} | all-to-all | bytes 1081344 | tf_op jit(solution)/shard_map/all_to_all | solution.py:328
  114.4 1.4 shard_map.77
  115.9 6.9 %collective-permute-start.2 = (s16[1032,128]{1,0:T(8,128)(2,1)S(1)}, s16[1032,128]{1,0:T(8,128)(2,1)S(1)}, u32[]{:S(2)}, u32[]{:S(2)}) collective-permute-start(s16[1032,128]{1,0:T(8,128)(2,1)S(1)} %get-tuple-element.52), channel_id=1, source_target_pairs={{0,1},{1,0},{2,3},{3,2},{4,5},{5,4},{6,7},{7,6},{8,9},{9,8},{10,11... | collective-permute-start | bytes 792584 | tf_op jit(solution)/shard_map/ppermute | solution.py:343
  122.7 1.2 shard_map.78.own_ref
  124.0 0.0 collective-permute-done.2.received_ref
  124.0 0.2 shard_map.79
  124.2 11.1 %all_to_all.66.refs_0_ = s16[16,72,128]{2,1,0:T(8,128)(2,1)S(1)} all-to-all(s16[16,72,128]{2,1,0:T(8,128)(2,1)S(1)} %shard_map.79), channel_id=1, replica_groups=mesh['row'=8,'col_0'=4,'col_1'=4,'col_2'=2] {'col_0','col_1'}, dimensions={0} | all-to-all | bytes 589824 | tf_op jit(solution)/shard_map/all_to_all | solution.py:328
  135.3 0.1 shard_map.80
  135.5 11.1 %all_to_all.67.own_ref = bf16[16,72,128]{2,1,0:T(8,128)(2,1)S(1)} all-to-all(bf16[16,72,128]{2,1,0:T(8,128)(2,1)S(1)} %get-tuple-element.55), channel_id=1, replica_groups=mesh['row'=8,'col_0'=4,'col_1'=4,'col_2'=2] {'col_0','col_1'}, dimensions={0} | all-to-all | bytes 589824 | tf_op jit(solution)/shard_map/all_to_all | solution.py:328
  146.6 2.9 %collective-permute-start.3 = (bf16[16,72,128]{2,1,0:T(8,128)(2,1)S(1)}, bf16[16,72,128]{2,1,0:T(8,128)(2,1)S(1)}, u32[]{:S(2)}, u32[]{:S(2)}) collective-permute-start(bf16[16,72,128]{2,1,0:T(8,128)(2,1)S(1)} %all_to_all.67.own_ref), channel_id=1, source_target_pairs={{0,1},{1,0},{2,3},{3,2},{4,5},{5,4},{6,7},{7,6},{8,9},{9,8},{10,11... | collective-permute-start | bytes 884744 | tf_op jit(solution)/shard_map/ppermute | solution.py:343
  149.4 0.8 shard_map.81
  150.2 0.4 collective-permute-done.3.other_ref
  150.7 1.2 shard_map.82
  151.9 14.6 %all_to_all.68.refs_0_ = s16[8,264,128]{2,1,0:T(8,128)(2,1)S(1)} all-to-all(s16[8,264,128]{2,1,0:T(8,128)(2,1)S(1)} %shard_map.82), channel_id=1, replica_groups=mesh['row'=8,'col_0'=4,'col_1'=4,'col_2'=2] {'row'}, dimensions={0} | all-to-all | bytes 1081344 | tf_op jit(solution)/shard_map/all_to_all | solution.py:328
  166.5 0.3 shard_map.83
  166.8 15.8 %all_to_all.69.voxels_ref.voxels2 = s16[8,264,128]{2,1,0:T(8,128)(2,1)S(1)} all-to-all(s16[8,264,128]{2,1,0:T(8,128)(2,1)S(1)} %get-tuple-element.60), channel_id=1, replica_groups=mesh['row'=8,'col_0'=4,'col_1'=4,'col_2'=2] {'row'}, dimensions={0} | all-to-all | bytes 1081344 | tf_op jit(solution)/shard_map/all_to_all | solution.py:328
  182.6 1.4 shard_map.84
  184.1 6.7 %collective-permute-start.4 = (s16[1032,128]{1,0:T(8,128)(2,1)S(1)}, s16[1032,128]{1,0:T(8,128)(2,1)S(1)}, u32[]{:S(2)}, u32[]{:S(2)}) collective-permute-start(s16[1032,128]{1,0:T(8,128)(2,1)S(1)} %get-tuple-element.63), channel_id=1, source_target_pairs={{0,1},{1,0},{2,3},{3,2},{4,5},{5,4},{6,7},{7,6},{8,9},{9,8},{10,11... | collective-permute-start | bytes 792584 | tf_op jit(solution)/shard_map/ppermute | solution.py:343
  190.8 1.2 shard_map.85.own_ref
  192.0 0.0 collective-permute-done.4.received_ref
  192.0 0.2 shard_map.86
  192.3 11.1 %all_to_all.70.refs_0_ = s16[16,72,128]{2,1,0:T(8,128)(2,1)S(1)} all-to-all(s16[16,72,128]{2,1,0:T(8,128)(2,1)S(1)} %shard_map.86), channel_id=1, replica_groups=mesh['row'=8,'col_0'=4,'col_1'=4,'col_2'=2] {'col_0','col_1'}, dimensions={0} | all-to-all | bytes 589824 | tf_op jit(solution)/shard_map/all_to_all | solution.py:328
  203.4 0.1 shard_map.87
  203.5 2.0 collective-permute-start.5
  205.4 0.8 collective-permute-done.5
  206.3 16.6 %all_to_all.71 = f32[128,1,128]{2,1,0:T(1,128)S(1)} all-to-all(f32[128,1,128]{2,1,0:T(1,128)S(1)} %broadcast_in_dim.9), channel_id=1, replica_groups=mesh['row'=8,'col_0'=4,'col_1'=4,'col_2'=2] {'row','col_0','col_1'}, dimensions={0} | all-to-all | bytes 131072 | tf_op jit(solution)/shard_map/all_to_all | solution.py:328
  223.0 1.7 shard_map.88
  (4 shorter events, 0.1 us)
Async XLA Ops:
  43.2 9.1 %collective-permute-start = (s16[1032,128]{1,0:T(8,128)(2,1)S(1)}, s16[1032,128]{1,0:T(8,128)(2,1)S(1)}, u32[]{:S(2)}, u32[]{:S(2)}) collective-permute-start(s16[1032,128]{1,0:T(8,128)(2,1)S(1)} %get-tuple-element.41), channel_id=1, source_target_pairs={{0,1},{1,0},{2,3},{3,2},{4,5},{5,4},{6,7},{7,6},{8,9},{9,8},{10,11... | collective-permute-start | bytes 792584 | tf_op jit(solution)/shard_map/ppermute | solution.py:343
  78.4 4.1 %collective-permute-start.1 = (bf16[16,72,128]{2,1,0:T(8,128)(2,1)S(1)}, bf16[16,72,128]{2,1,0:T(8,128)(2,1)S(1)}, u32[]{:S(2)}, u32[]{:S(2)}) collective-permute-start(bf16[16,72,128]{2,1,0:T(8,128)(2,1)S(1)} %all_to_all.63.own_ref), channel_id=1, source_target_pairs={{0,1},{1,0},{2,3},{3,2},{4,5},{5,4},{6,7},{7,6},{8,9},{9,8},{10,11... | collective-permute-start | bytes 884744 | tf_op jit(solution)/shard_map/ppermute | solution.py:343
  115.9 8.1 %collective-permute-start.2 = (s16[1032,128]{1,0:T(8,128)(2,1)S(1)}, s16[1032,128]{1,0:T(8,128)(2,1)S(1)}, u32[]{:S(2)}, u32[]{:S(2)}) collective-permute-start(s16[1032,128]{1,0:T(8,128)(2,1)S(1)} %get-tuple-element.52), channel_id=1, source_target_pairs={{0,1},{1,0},{2,3},{3,2},{4,5},{5,4},{6,7},{7,6},{8,9},{9,8},{10,11... | collective-permute-start | bytes 792584 | tf_op jit(solution)/shard_map/ppermute | solution.py:343
  146.6 4.1 %collective-permute-start.3 = (bf16[16,72,128]{2,1,0:T(8,128)(2,1)S(1)}, bf16[16,72,128]{2,1,0:T(8,128)(2,1)S(1)}, u32[]{:S(2)}, u32[]{:S(2)}) collective-permute-start(bf16[16,72,128]{2,1,0:T(8,128)(2,1)S(1)} %all_to_all.67.own_ref), channel_id=1, source_target_pairs={{0,1},{1,0},{2,3},{3,2},{4,5},{5,4},{6,7},{7,6},{8,9},{9,8},{10,11... | collective-permute-start | bytes 884744 | tf_op jit(solution)/shard_map/ppermute | solution.py:343
  184.1 8.0 %collective-permute-start.4 = (s16[1032,128]{1,0:T(8,128)(2,1)S(1)}, s16[1032,128]{1,0:T(8,128)(2,1)S(1)}, u32[]{:S(2)}, u32[]{:S(2)}) collective-permute-start(s16[1032,128]{1,0:T(8,128)(2,1)S(1)} %get-tuple-element.63), channel_id=1, source_target_pairs={{0,1},{1,0},{2,3},{3,2},{4,5},{5,4},{6,7},{7,6},{8,9},{9,8},{10,11... | collective-permute-start | bytes 792584 | tf_op jit(solution)/shard_map/ppermute | solution.py:343
  203.5 2.8 %collective-permute-start.5 = (f32[1,128]{1,0:T(1,128)S(1)}, f32[1,128]{1,0:T(1,128)S(1)}, u32[]{:S(2)}, u32[]{:S(2)}) collective-permute-start(f32[1,128]{1,0:T(1,128)S(1)} %get-tuple-element.67), channel_id=1, source_target_pairs={{0,1},{1,0},{2,3},{3,2},{4,5},{5,4},{6,7},{7,6},{8,9},{9,8},{10,11... | collective-permute-start | bytes 1544 | tf_op jit(solution)/shard_map/ppermute | solution.py:343

commit v5 on v4

--- a/solution.py
+++ b/solution.py
@@ -7,7 +7,7 @@
 from jax.sharding import PartitionSpec as P
 
 TILE = 128
-WIDTH = 256
+WIDTH = 512
 CHUNKS = 4
 ITERS = 3
 EPSILON = 1e-06

time: 225 us -> 225 us (level)
  no operation moved by 1% of the time
where the time goes in v5:
time: 225 us
  blocking collectives  173 us (77%)
  starting transfers between devices  29.1 us (13%)
  Pallas kernels  20 us (9%)
    all_to_all x12, blocking collectives, exchanged(): return lax.all_to_all(array, axis, 0, 0, tiled=True)  173 us
    ppermute x6, starting transfers between devices, swapped(): return lax.ppermute(array, 'col_2', [(0, 1), (1, 0)])  29.1 us
    pallas_call x20, Pallas kernels, call(): pl.pallas_call(kernel, in_specs=[whole(pltpu.SMEM)] * scalars + [whole()]...  15.7 us
  transfers between devices with their start and end apart: 6, of which 3 were waited for; matrix products, arithmetic and copies ran while one was open for 0% of the time, Pallas kernels for 2%

profile of v5, /device:TPU:1, one launch (start us, length us, event | category | flops | bytes accessed | tf_op | source)
XLA Modules:
  0.0 224.9 jit_solution(17162977042395916967)
XLA Ops:
  1.3 4.3 %shard_map.68 = (bf16[2048,2048]{1,0:T(8,128)(2,1)S(1)}, s16[8,264,128]{2,1,0:T(8,128)(2,1)S(1)}, f32[64,128]{1,0:T(8,128)S(1)}) custom-call(s32[1]{0:T(128)} %bitcast.start_ref, s32[1]{0:T(128)} %bitcast.9.count_ref, s32[1,1,128]{2,1,0:T(1,128)} %rows_ref.1, s32[1,1,128]{2,1,0:T(1,128)} %cols_ref.1, bf16[1,1,128,128,128]{4,3,2,1,0:T(8,128)(2,1)} %tiles_ref.1, ...), custom_call_target="tpu_custom_call" | custom-call | tf_op jit(solution)/shard_map/pallas_call | solution.py:351
  5.6 21.1 %all_to_all.60.refs_0_ = s16[8,264,128]{2,1,0:T(8,128)(2,1)S(1)} all-to-all(s16[8,264,128]{2,1,0:T(8,128)(2,1)S(1)} %get-tuple-element.36), channel_id=1, replica_groups=mesh['row'=8,'col_0'=4,'col_1'=4,'col_2'=2] {'row'}, dimensions={0} | all-to-all | bytes 1081344 | tf_op jit(solution)/shard_map/all_to_all | solution.py:328
  26.7 0.3 shard_map.69
  27.0 14.7 %all_to_all.61.voxels_ref.voxels0 = s16[8,264,128]{2,1,0:T(8,128)(2,1)S(1)} all-to-all(s16[8,264,128]{2,1,0:T(8,128)(2,1)S(1)} %get-tuple-element.37), channel_id=1, replica_groups=mesh['row'=8,'col_0'=4,'col_1'=4,'col_2'=2] {'row'}, dimensions={0} | all-to-all | bytes 1081344 | tf_op jit(solution)/shard_map/all_to_all | solution.py:328
  41.7 1.4 shard_map.70
  43.1 7.9 %collective-permute-start = (s16[1032,128]{1,0:T(8,128)(2,1)S(1)}, s16[1032,128]{1,0:T(8,128)(2,1)S(1)}, u32[]{:S(2)}, u32[]{:S(2)}) collective-permute-start(s16[1032,128]{1,0:T(8,128)(2,1)S(1)} %get-tuple-element.41), channel_id=1, source_target_pairs={{0,1},{1,0},{2,3},{3,2},{4,5},{5,4},{6,7},{7,6},{8,9},{9,8},{10,11... | collective-permute-start | bytes 792584 | tf_op jit(solution)/shard_map/ppermute | solution.py:343
  51.0 1.2 shard_map.71.own_ref
  52.3 0.0 collective-permute-done.received_ref
  52.3 0.2 shard_map.72
  52.5 14.8 %all_to_all.62.refs_0_ = s16[16,72,128]{2,1,0:T(8,128)(2,1)S(1)} all-to-all(s16[16,72,128]{2,1,0:T(8,128)(2,1)S(1)} %shard_map.72), channel_id=1, replica_groups=mesh['row'=8,'col_0'=4,'col_1'=4,'col_2'=2] {'col_0','col_1'}, dimensions={0} | all-to-all | bytes 589824 | tf_op jit(solution)/shard_map/all_to_all | solution.py:328
  67.3 0.1 shard_map.73
  67.5 11.1 %all_to_all.63.own_ref = bf16[16,72,128]{2,1,0:T(8,128)(2,1)S(1)} all-to-all(bf16[16,72,128]{2,1,0:T(8,128)(2,1)S(1)} %get-tuple-element.44), channel_id=1, replica_groups=mesh['row'=8,'col_0'=4,'col_1'=4,'col_2'=2] {'col_0','col_1'}, dimensions={0} | all-to-all | bytes 589824 | tf_op jit(solution)/shard_map/all_to_all | solution.py:328
  78.6 2.9 %collective-permute-start.1 = (bf16[16,72,128]{2,1,0:T(8,128)(2,1)S(1)}, bf16[16,72,128]{2,1,0:T(8,128)(2,1)S(1)}, u32[]{:S(2)}, u32[]{:S(2)}) collective-permute-start(bf16[16,72,128]{2,1,0:T(8,128)(2,1)S(1)} %all_to_all.63.own_ref), channel_id=1, source_target_pairs={{0,1},{1,0},{2,3},{3,2},{4,5},{5,4},{6,7},{7,6},{8,9},{9,8},{10,11... | collective-permute-start | bytes 884744 | tf_op jit(solution)/shard_map/ppermute | solution.py:343
  81.5 0.8 shard_map.74
  82.3 0.4 collective-permute-done.1.other_ref
  82.7 1.2 shard_map.75
  83.9 14.6 %all_to_all.64.refs_0_ = s16[8,264,128]{2,1,0:T(8,128)(2,1)S(1)} all-to-all(s16[8,264,128]{2,1,0:T(8,128)(2,1)S(1)} %shard_map.75), channel_id=1, replica_groups=mesh['row'=8,'col_0'=4,'col_1'=4,'col_2'=2] {'row'}, dimensions={0} | all-to-all | bytes 1081344 | tf_op jit(solution)/shard_map/all_to_all | solution.py:328
  98.5 0.3 shard_map.76
  98.8 15.8 %all_to_all.65.voxels_ref.voxels1 = s16[8,264,128]{2,1,0:T(8,128)(2,1)S(1)} all-to-all(s16[8,264,128]{2,1,0:T(8,128)(2,1)S(1)} %get-tuple-element.49), channel_id=1, replica_groups=mesh['row'=8,'col_0'=4,'col_1'=4,'col_2'=2] {'row'}, dimensions={0} | all-to-all | bytes 1081344 | tf_op jit(solution)/shard_map/all_to_all | solution.py:328
  114.6 1.4 shard_map.77
  116.1 6.9 %collective-permute-start.2 = (s16[1032,128]{1,0:T(8,128)(2,1)S(1)}, s16[1032,128]{1,0:T(8,128)(2,1)S(1)}, u32[]{:S(2)}, u32[]{:S(2)}) collective-permute-start(s16[1032,128]{1,0:T(8,128)(2,1)S(1)} %get-tuple-element.52), channel_id=1, source_target_pairs={{0,1},{1,0},{2,3},{3,2},{4,5},{5,4},{6,7},{7,6},{8,9},{9,8},{10,11... | collective-permute-start | bytes 792584 | tf_op jit(solution)/shard_map/ppermute | solution.py:343
  123.0 1.2 shard_map.78.own_ref
  124.2 0.0 collective-permute-done.2.received_ref
  124.2 0.2 shard_map.79
  124.5 11.1 %all_to_all.66.refs_0_ = s16[16,72,128]{2,1,0:T(8,128)(2,1)S(1)} all-to-all(s16[16,72,128]{2,1,0:T(8,128)(2,1)S(1)} %shard_map.79), channel_id=1, replica_groups=mesh['row'=8,'col_0'=4,'col_1'=4,'col_2'=2] {'col_0','col_1'}, dimensions={0} | all-to-all | bytes 589824 | tf_op jit(solution)/shard_map/all_to_all | solution.py:328
  135.6 0.1 shard_map.80
  135.7 11.1 %all_to_all.67.own_ref = bf16[16,72,128]{2,1,0:T(8,128)(2,1)S(1)} all-to-all(bf16[16,72,128]{2,1,0:T(8,128)(2,1)S(1)} %get-tuple-element.55), channel_id=1, replica_groups=mesh['row'=8,'col_0'=4,'col_1'=4,'col_2'=2] {'col_0','col_1'}, dimensions={0} | all-to-all | bytes 589824 | tf_op jit(solution)/shard_map/all_to_all | solution.py:328
  146.8 2.9 %collective-permute-start.3 = (bf16[16,72,128]{2,1,0:T(8,128)(2,1)S(1)}, bf16[16,72,128]{2,1,0:T(8,128)(2,1)S(1)}, u32[]{:S(2)}, u32[]{:S(2)}) collective-permute-start(bf16[16,72,128]{2,1,0:T(8,128)(2,1)S(1)} %all_to_all.67.own_ref), channel_id=1, source_target_pairs={{0,1},{1,0},{2,3},{3,2},{4,5},{5,4},{6,7},{7,6},{8,9},{9,8},{10,11... | collective-permute-start | bytes 884744 | tf_op jit(solution)/shard_map/ppermute | solution.py:343
  149.7 0.8 shard_map.81
  150.5 0.4 collective-permute-done.3.other_ref
  150.9 1.2 shard_map.82
  152.1 14.6 %all_to_all.68.refs_0_ = s16[8,264,128]{2,1,0:T(8,128)(2,1)S(1)} all-to-all(s16[8,264,128]{2,1,0:T(8,128)(2,1)S(1)} %shard_map.82), channel_id=1, replica_groups=mesh['row'=8,'col_0'=4,'col_1'=4,'col_2'=2] {'row'}, dimensions={0} | all-to-all | bytes 1081344 | tf_op jit(solution)/shard_map/all_to_all | solution.py:328
  166.7 0.3 shard_map.83
  167.0 15.8 %all_to_all.69.voxels_ref.voxels2 = s16[8,264,128]{2,1,0:T(8,128)(2,1)S(1)} all-to-all(s16[8,264,128]{2,1,0:T(8,128)(2,1)S(1)} %get-tuple-element.60), channel_id=1, replica_groups=mesh['row'=8,'col_0'=4,'col_1'=4,'col_2'=2] {'row'}, dimensions={0} | all-to-all | bytes 1081344 | tf_op jit(solution)/shard_map/all_to_all | solution.py:328
  182.9 1.4 shard_map.84
  184.3 6.7 %collective-permute-start.4 = (s16[1032,128]{1,0:T(8,128)(2,1)S(1)}, s16[1032,128]{1,0:T(8,128)(2,1)S(1)}, u32[]{:S(2)}, u32[]{:S(2)}) collective-permute-start(s16[1032,128]{1,0:T(8,128)(2,1)S(1)} %get-tuple-element.63), channel_id=1, source_target_pairs={{0,1},{1,0},{2,3},{3,2},{4,5},{5,4},{6,7},{7,6},{8,9},{9,8},{10,11... | collective-permute-start | bytes 792584 | tf_op jit(solution)/shard_map/ppermute | solution.py:343
  191.0 1.2 shard_map.85.own_ref
  192.3 0.0 collective-permute-done.4.received_ref
  192.3 0.2 shard_map.86
  192.5 11.1 %all_to_all.70.refs_0_ = s16[16,72,128]{2,1,0:T(8,128)(2,1)S(1)} all-to-all(s16[16,72,128]{2,1,0:T(8,128)(2,1)S(1)} %shard_map.86), channel_id=1, replica_groups=mesh['row'=8,'col_0'=4,'col_1'=4,'col_2'=2] {'col_0','col_1'}, dimensions={0} | all-to-all | bytes 589824 | tf_op jit(solution)/shard_map/all_to_all | solution.py:328
  203.6 0.1 shard_map.87
  203.7 2.0 collective-permute-start.5
  205.7 0.8 collective-permute-done.5
  206.5 16.6 %all_to_all.71 = f32[128,1,128]{2,1,0:T(1,128)S(1)} all-to-all(f32[128,1,128]{2,1,0:T(1,128)S(1)} %broadcast_in_dim.9), channel_id=1, replica_groups=mesh['row'=8,'col_0'=4,'col_1'=4,'col_2'=2] {'row','col_0','col_1'}, dimensions={0} | all-to-all | bytes 131072 | tf_op jit(solution)/shard_map/all_to_all | solution.py:328
  223.2 1.7 shard_map.88
  (4 shorter events, 0.1 us)
Async XLA Ops:
  43.1 9.1 %collective-permute-start = (s16[1032,128]{1,0:T(8,128)(2,1)S(1)}, s16[1032,128]{1,0:T(8,128)(2,1)S(1)}, u32[]{:S(2)}, u32[]{:S(2)}) collective-permute-start(s16[1032,128]{1,0:T(8,128)(2,1)S(1)} %get-tuple-element.41), channel_id=1, source_target_pairs={{0,1},{1,0},{2,3},{3,2},{4,5},{5,4},{6,7},{7,6},{8,9},{9,8},{10,11... | collective-permute-start | bytes 792584 | tf_op jit(solution)/shard_map/ppermute | solution.py:343
  78.6 4.1 %collective-permute-start.1 = (bf16[16,72,128]{2,1,0:T(8,128)(2,1)S(1)}, bf16[16,72,128]{2,1,0:T(8,128)(2,1)S(1)}, u32[]{:S(2)}, u32[]{:S(2)}) collective-permute-start(bf16[16,72,128]{2,1,0:T(8,128)(2,1)S(1)} %all_to_all.63.own_ref), channel_id=1, source_target_pairs={{0,1},{1,0},{2,3},{3,2},{4,5},{5,4},{6,7},{7,6},{8,9},{9,8},{10,11... | collective-permute-start | bytes 884744 | tf_op jit(solution)/shard_map/ppermute | solution.py:343
  116.1 8.1 %collective-permute-start.2 = (s16[1032,128]{1,0:T(8,128)(2,1)S(1)}, s16[1032,128]{1,0:T(8,128)(2,1)S(1)}, u32[]{:S(2)}, u32[]{:S(2)}) collective-permute-start(s16[1032,128]{1,0:T(8,128)(2,1)S(1)} %get-tuple-element.52), channel_id=1, source_target_pairs={{0,1},{1,0},{2,3},{3,2},{4,5},{5,4},{6,7},{7,6},{8,9},{9,8},{10,11... | collective-permute-start | bytes 792584 | tf_op jit(solution)/shard_map/ppermute | solution.py:343
  146.8 4.1 %collective-permute-start.3 = (bf16[16,72,128]{2,1,0:T(8,128)(2,1)S(1)}, bf16[16,72,128]{2,1,0:T(8,128)(2,1)S(1)}, u32[]{:S(2)}, u32[]{:S(2)}) collective-permute-start(bf16[16,72,128]{2,1,0:T(8,128)(2,1)S(1)} %all_to_all.67.own_ref), channel_id=1, source_target_pairs={{0,1},{1,0},{2,3},{3,2},{4,5},{5,4},{6,7},{7,6},{8,9},{9,8},{10,11... | collective-permute-start | bytes 884744 | tf_op jit(solution)/shard_map/ppermute | solution.py:343
  184.3 7.9 %collective-permute-start.4 = (s16[1032,128]{1,0:T(8,128)(2,1)S(1)}, s16[1032,128]{1,0:T(8,128)(2,1)S(1)}, u32[]{:S(2)}, u32[]{:S(2)}) collective-permute-start(s16[1032,128]{1,0:T(8,128)(2,1)S(1)} %get-tuple-element.63), channel_id=1, source_target_pairs={{0,1},{1,0},{2,3},{3,2},{4,5},{5,4},{6,7},{7,6},{8,9},{9,8},{10,11... | collective-permute-start | bytes 792584 | tf_op jit(solution)/shard_map/ppermute | solution.py:343
  203.7 2.8 %collective-permute-start.5 = (f32[1,128]{1,0:T(1,128)S(1)}, f32[1,128]{1,0:T(1,128)S(1)}, u32[]{:S(2)}, u32[]{:S(2)}) collective-permute-start(f32[1,128]{1,0:T(1,128)S(1)} %get-tuple-element.67), channel_id=1, source_target_pairs={{0,1},{1,0},{2,3},{3,2},{4,5},{5,4},{6,7},{7,6},{8,9},{9,8},{10,11... | collective-permute-start | bytes 1544 | tf_op jit(solution)/shard_map/ppermute | solution.py:343
